TPU v7x, 128 devices: a whole 4x4x4 slice. The times are simulated.
128 devices in a mesh: cuts: 8 (over z, x_lo), row: 16 (over x_hi, y, core).
Axes of the slice: x: 4 (x_hi: 2, x_lo: 2; x = x_hi * 2 + x_lo), y: 4, z: 4, core: 2. Of those that a mesh axis runs over, the one named last changes fastest.
Arguments:
- eigvecs: float32 [16384, 4096], P('row', 'cuts'), may hold values from -1.2 to 1.2
- slice_counts: int32 [8], P('cuts'), may hold values from 256 to 512, as said below
- occ_index: int32 [4096], P('cuts'), may hold values from 0 to 63
- occ_levels: float32 [64], replicated, may hold values from 0 to 1
Outputs:
- slab: float32 [4096, 16384], P('cuts', 'row')
Inputs may be any that keep to these rules, and one draw needn't show every extreme that they name: `slice_counts`: some slice holds exactly 512 eigenvalues in every draw; the others at least half of that.
All inputs are finite; a program needn't handle non-finite values.
Results may differ from a plain program's by a relative error of at most 0.000062.
Values sent between devices are 32-bit elements; how exact they have to be, the bound alone decides.
A program may use at most 128 MiB of HBM per device.

v0:
```python
import jax
import jax.numpy as jnp
from jax import lax
from jax.sharding import Mesh
from jax.sharding import PartitionSpec as P

BLOCK = 1024
SLAB_SUB = 256
CUTS = ("cuts_0", "cuts_1")


def sum_by_axis(total, axes):
    for axis in axes:
        total = lax.psum_scatter(total, axis, scatter_dimension=0, tiled=True)
    return total


def shards(eigvecs, slice_counts, occ_index, occ_levels):
    row_count = eigvecs.shape[0]
    slot_count = eigvecs.shape[1]
    level_ids = jnp.arange(occ_levels.shape[0], dtype=jnp.int32)
    one_hot = (occ_index[:, None] == level_ids[None, :]).astype(jnp.float32)
    values = jnp.dot(one_hot, occ_levels, precision=lax.Precision.HIGHEST)
    live = jnp.arange(slot_count, dtype=jnp.int32) < slice_counts[0]
    weights = jnp.where(live, values, jnp.float32(0.0))
    local_blocks = eigvecs.reshape(row_count // BLOCK, BLOCK, slot_count)[:, :SLAB_SUB, :]
    local_rows = local_blocks.reshape(-1, slot_count) * weights[None, :]
    gathered = lax.all_gather(local_rows, "row", axis=0, tiled=True)
    return sum_by_axis(
        lax.dot_general(
            gathered,
            eigvecs,
            (((1,), (1,)), ((), ())),
            precision=lax.Precision.HIGHEST,
            preferred_element_type=jnp.float32,
        ),
        CUTS,
    )


def solution(mesh):
    finer = Mesh(mesh.devices.reshape(4, 2, mesh.shape["row"]), ("cuts_0", "cuts_1", "row"))
    in_specs = (P("row", CUTS), P(CUTS), P(CUTS), P())
    out_specs = P(CUTS, "row")
    return jax.shard_map(
        shards, mesh=finer, in_specs=in_specs, out_specs=out_specs, check_vma=False
    )
```

profile of v0, /device:TPU:1, one launch (start us, length us, event | category | flops | bytes accessed | tf_op | source)
XLA Modules:
  0.0 329.1 jit_solution(11867658746482311696)
XLA Ops:
  6.5 0.0 copy-start
  6.5 0.0 all-gather.2.cloned.1.call-start
  7.2 0.0 copy-done
  7.2 1.0 fusion.1
  8.2 1.9 fusion
  10.1 0.0 all-gather.2.cloned.1.call-update
  10.1 0.0 reduce-scatter.3.cloned.1.call-start
  10.2 76.3 %all-gather.2.cloned.1.call-done = f32[4096,512]{1,0:T(8,128)} async-done(((f32[256,512]{1,0:T(8,128)}), f32[4096,512]{1,0:T(8,128)}) %all-gather.2.cloned.1.call-update) | async-done | bytes 8388624 | tf_op jit(solution)/shard_map/all_gather | solution.py:28
  86.4 31.7 %fusion.5 = f32[4096,1024]{1,0:T(8,128)} fusion(f32[4096,512]{1,0:T(8,128)} %all-gather.2.cloned.1.call-done, f32[1024,512]{1,0:T(8,128)} %param.4), kind=kOutput, calls=%fused_computation.8 | convolution fusion | flops 25769803776 | bytes 27262976 | tf_op jit(solution)/shard_map/dot_general | solution.py:30
  118.1 0.0 reduce-scatter.3.cloned.1.call-update
  118.1 0.0 reduce-scatter.5.cloned.1.call-start
  118.2 145.6 %reduce-scatter.3.cloned.1.call-done = f32[1024,1024]{1,0:T(8,128)} async-done(((f32[4096,1024]{1,0:T(8,128)}), f32[1024,1024]{1,0:T(8,128)}) %reduce-scatter.3.cloned.1.call-update) | async-done | bytes 4194320 | tf_op jit(solution)/shard_map/reduce_scatter | solution.py:14
  263.8 0.0 reduce-scatter.5.cloned.1.call-update
  263.8 58.8 %reduce-scatter.5.cloned.1.call-done = f32[512,1024]{1,0:T(8,128)} async-done(((f32[1024,1024]{1,0:T(8,128)}), f32[512,1024]{1,0:T(8,128)}) %reduce-scatter.5.cloned.1.call-update) | async-done | bytes 2097168 | tf_op jit(solution)/shard_map/reduce_scatter | solution.py:14
  (1 shorter events, 0.0 us)
Async XLA Ops:
  6.5 0.7 copy-start
  6.5 79.9 %all-gather.2.cloned.1.call-start = ((), (), s32[]{:S(2)}) async-start(), calls=%async_computation.2 | async-start | bytes 8912896 | tf_op jit(solution)/shard_map/all_gather | solution.py:28
  10.1 253.7 %reduce-scatter.3.cloned.1.call-start = ((), (), s32[]{:S(2)}) async-start(), calls=%async_computation.3 | async-start | bytes 20971520 | tf_op jit(solution)/shard_map/reduce_scatter | solution.py:14
  118.1 204.5 %reduce-scatter.5.cloned.1.call-start = ((), (), s32[]{:S(2)}) async-start(), calls=%async_computation.4 | async-start | bytes 6291456 | tf_op jit(solution)/shard_map/reduce_scatter | solution.py:14
Sparse Core Ops, SparseCore 0:
  10.2 76.1 all-gather.1
  118.3 145.5 reduce-scatter.2
  266.2 56.3 reduce-scatter.4
where the time goes:
time: 329 us
  waiting for transfers between devices  281 us (85%)
  matrix products  32.7 us (10%)
  between operations  13.8 us (4%)
    reduce_scatter x2, waiting for transfers between devices, sum_by_axis(): total = lax.psum_scatter(total, axis, scatter_dimension=0, tiled=True)  204 us
    all_gather x1, waiting for transfers between devices, shards(): gathered = lax.all_gather(local_rows, 'row', axis=0, tiled=True)  76.3 us
    dot_general x1, matrix products, shards(): lax.dot_general(gathered, eigvecs, (((1,), (1,)), ((), ())), precision=la...  31.7 us
  transfers between devices with their start and end apart: 3, of which 3 were waited for; matrix products, arithmetic and copies ran while one was open for 0% of the time, Pallas kernels for 0%

commit v1 on v0

v1 whole, which is shorter than its diff:
```python
import jax
import jax.numpy as jnp
from jax import lax
from jax.experimental import pallas as pl
from jax.experimental.pallas import tpu as pltpu
from jax.sharding import PartitionSpec as P

MESH = pl.DeviceIdType.MESH
SUB = 256
HALVES = 2
HROWS = SUB // HALVES
CHUNKS = 4
F32, BF16 = jnp.float32, jnp.bfloat16


def split(value):
    high = value.astype(BF16)
    return high, (value - high.astype(F32)).astype(BF16)


def kernel(
    e_ref, idx_ref, lev_ref, cnt_ref, out_ref,
    p_buf, own_p, e_in, p_hi, p_lo, e_hi, e_lo, part, zin,
    xs_sem, ys_sem, cs_sem, p_sem, es_sem, er_sem, as_sem, ar_sem, zs_sem, zr_sem,
):
    rows, depth = e_ref.shape
    width = rows // CHUNKS
    c, r = lax.axis_index("cuts"), lax.axis_index("row")
    z, xl = c // 2, lax.rem(c, 2)
    q, core = r // 2, lax.rem(r, 2)
    xh, y = q // 4, lax.rem(q, 4)
    x = xh * 2 + xl

    def device(dx=0, dy=0, dz=0, dcore=0):
        nx, ny = lax.rem(x + dx + 4, 4), lax.rem(y + dy + 4, 4)
        nz, ncore = lax.rem(z + dz + 4, 4), lax.rem(core + dcore, 2)
        return (nz * 2 + lax.rem(nx, 2), ((nx // 2) * 4 + ny) * 2 + ncore)

    pair = (z * 2 + 1 - xl, r)
    source = lax.rem(y, 2) == xl
    own_rel = lax.rem(2 * xh + y // 2 - z + 4, 4)
    even_row = y // 2 == lax.rem(z, 2)

    def row_gap(rel):
        return lax.rem(2 * lax.rem(z + rel, 2) + xl - y + 4, 4)

    barrier = pltpu.get_barrier_semaphore()
    for peer in (
        device(dx=1), device(dx=2), device(dx=3), device(dy=1), device(dy=3),
        device(dz=1), device(dz=3), device(dcore=1),
    ):
        pl.semaphore_signal(barrier, inc=1, device_id=peer, device_id_type=MESH)

    level = lax.broadcasted_iota(jnp.int32, (lev_ref.shape[0], depth), 0)
    chosen = jnp.where(level == idx_ref[...], lev_ref[...], F32(0.0))
    values = jnp.sum(chosen, axis=0, keepdims=True)
    live = lax.broadcasted_iota(jnp.int32, (1, depth), 1) < cnt_ref[0]
    weights = jnp.where(live, values, F32(0.0))
    for h in range(HALVES):
        own_p[h] = e_ref[h * HROWS : (h + 1) * HROWS, :] * weights

    @pl.when(source)
    def _():
        for h in range(HALVES):
            p_buf[own_rel, core, 0, h] = own_p[h]

    pl.semaphore_wait(barrier, 8)

    def copy(src, dst, send, recv, peer):
        return pltpu.make_async_remote_copy(
            src_ref=src, dst_ref=dst, send_sem=send, recv_sem=recv,
            device_id=peer, device_id_type=MESH,
        )

    def x_copy(h, side, s, peer):
        slot = p_buf.at[own_rel, core, s, h]
        return copy(own_p.at[h], slot, xs_sem.at[side, h], p_sem.at[own_rel, core, s, h], peer)

    def y_copy(rel, s, h, up):
        slot = p_buf.at[rel, core, s, h]
        side = 0 if up else 1
        return copy(
            slot, slot, ys_sem.at[side, rel, s, h], p_sem.at[rel, core, s, h],
            device(dy=1 if up else 3),
        )

    def core_copy(rel, s, h):
        slot = p_buf.at[rel, core, s, h]
        return copy(slot, slot, cs_sem.at[rel, s, h], p_sem.at[rel, core, s, h], device(dcore=1))

    def e_copy(j):
        return copy(
            e_ref.at[pl.ds(j * width, width)], e_in.at[j], es_sem.at[j], er_sem.at[j], pair
        )

    for h in range(HALVES):
        @pl.when(source)
        def _():
            x_copy(h, 0, 0, device(dx=2)).start()

        @pl.when(jnp.logical_not(source))
        def _():
            x_copy(h, 0, 1, device(dx=1)).start()
            x_copy(h, 1, 1, device(dx=3)).start()
    for j in range(CHUNKS):
        e_copy(j).start()

    for j in range(CHUNKS):
        span = pl.ds(j * width, width)
        high, low = split(e_ref[span, :])
        e_hi[span, :depth] = high
        e_lo[span, :depth] = low

    def arrive(rel, k, s, h):
        slot = p_buf.at[rel, k, s, h]
        pltpu.make_async_copy(slot, slot, p_sem.at[rel, k, s, h]).wait()

    def keep(rel, k, s, h):
        high, low = split(p_buf[rel, k, s, h])
        rows_of = pl.ds(h * HROWS, HROWS)
        p_hi[rel, k, rows_of, s * depth : (s + 1) * depth] = high
        p_lo[rel, k, rows_of, s * depth : (s + 1) * depth] = low

    def sends_up(rel, s):
        gap = row_gap(rel)
        return (gap == 0) | (gap == 3) if s == 0 else gap == 0

    def sends_down(rel, s):
        gap = row_gap(rel)
        return (gap == 0) | (gap == 1) if s == 1 else gap == 0

    def relay(rel, s, h):
        mine = source & (rel == own_rel) if s == 0 else None

        def take():
            arrive(rel, core, s, h)

        if mine is None:
            take()
        else:
            pl.when(jnp.logical_not(mine))(take)

        @pl.when(sends_up(rel, s))
        def _():
            y_copy(rel, s, h, True).start()

        @pl.when(sends_down(rel, s))
        def _():
            y_copy(rel, s, h, False).start()

        core_copy(rel, s, h).start()
        keep(rel, core, s, h)

    @pl.when(source)
    def _():
        for even, odd in (((2, 0), (1, 0)), ((2, 1), (3, 0)), ((0, 0), (1, 1)), ((0, 1), (3, 1))):
            rel = jnp.where(even_row, even[0], odd[0])
            h = jnp.where(even_row, even[1], odd[1])
            for s in range(2):
                relay(rel, s, h)

    def get_block(rel, h):
        @pl.when(jnp.logical_not(source & (row_gap(rel) == 0)))
        def _():
            for s in range(2):
                relay(rel, s, h)

        for s in range(2):
            arrive(rel, 1 - core, s, h)
            keep(rel, 1 - core, s, h)

    def get_rows(j):
        e_copy(j).wait_recv()
        span = pl.ds(j * width, width)
        high, low = split(e_in[j])
        e_hi[span, depth:] = high
        e_lo[span, depth:] = low

    def dot(a, b):
        return lax.dot_general(a, b, (((1,), (1,)), ((), ())), preferred_element_type=F32)

    def tile(rel, k, rows_of, j):
        span = pl.ds(j * width, width)
        high, low = p_hi[rel, k, rows_of, :], p_lo[rel, k, rows_of, :]
        e_high, e_low = e_hi[span, :], e_lo[span, :]
        return dot(high, e_high) + (dot(high, e_low) + dot(low, e_high))

    def ring(way):
        nz = lax.rem(z + 1 + 2 * way, 4)
        return (nz * 2 + xl, r)

    def first_copy(way, h, j):
        rows_of = pl.ds(h * HROWS, HROWS)
        return copy(
            part.at[0, way, j, rows_of], zin.at[0, way, j, rows_of],
            as_sem.at[way, h, j], ar_sem.at[way, h, j], ring(way),
        )

    def later_copy(kind, way, j):
        return copy(
            part.at[kind, way, j], zin.at[kind, way, j],
            zs_sem.at[kind - 1, way, j], zr_sem.at[kind - 1, way, j], ring(way),
        )

    def first(h, j):
        def body(way, carry):
            rows_of = pl.ds(h * HROWS, HROWS)
            part[0, way, j, rows_of] = tile(2, way, rows_of, j)
            first_copy(way, h, j).start()
            return carry

        lax.fori_loop(0, 2, body, 0)

    def second(j):
        def body(way, carry):
            part[1, way, j] = tile(1 + 2 * way, 1 - way, pl.ds(0, SUB), j)
            later_copy(1, way, j).start()
            return carry

        lax.fori_loop(0, 2, body, 0)

    def third(j):
        def body(way, carry):
            total = tile(1 + 2 * way, way, pl.ds(0, SUB), j)
            for h in range(HALVES):
                first_copy(way, h, j).wait_recv()
            part[2, way, j] = total + zin[0, way, j]
            later_copy(2, way, j).start()
            return carry

        lax.fori_loop(0, 2, body, 0)

    def last(j):
        def body(k, carry):
            rows_of = pl.ds(k * SUB, SUB)
            out_ref[rows_of, j * width : (j + 1) * width] = tile(0, k, pl.ds(0, SUB), j)
            return carry

        lax.fori_loop(0, 2, body, 0)

    def finish(j):
        def body(k, carry):
            rows_of = pl.ds(k * SUB, SUB)
            later_copy(1, 1 - k, j).wait_recv()
            later_copy(2, k, j).wait_recv()
            out_ref[rows_of, j * width : (j + 1) * width] += zin[2, k, j] + zin[1, 1 - k, j]
            return carry

        lax.fori_loop(0, 2, body, 0)

    get_block(2, 0)
    get_rows(0)
    first(0, 0)
    get_block(2, 1)
    first(1, 0)
    get_rows(1)
    first(0, 1)
    first(1, 1)
    get_block(1, 0)
    get_block(3, 0)
    get_block(1, 1)
    get_block(3, 1)
    second(0)
    third(0)
    get_block(0, 0)
    get_block(0, 1)
    second(1)
    third(1)
    get_rows(2)
    first(0, 2)
    first(1, 2)
    second(2)
    third(2)
    get_rows(3)
    first(0, 3)
    first(1, 3)
    second(3)
    third(3)
    for j in range(CHUNKS):
        last(j)
    for j in range(CHUNKS):
        finish(j)

    for h in range(HALVES):
        @pl.when(source)
        def _():
            x_copy(h, 0, 0, device(dx=2)).wait_send()

        @pl.when(jnp.logical_not(source))
        def _():
            x_copy(h, 0, 1, device(dx=1)).wait_send()
            x_copy(h, 1, 1, device(dx=3)).wait_send()
    for j in range(CHUNKS):
        e_copy(j).wait_send()
    for rel in range(4):
        for s in range(2):
            for h in range(HALVES):
                @pl.when(sends_up(rel, s))
                def _():
                    y_copy(rel, s, h, True).wait_send()

                @pl.when(sends_down(rel, s))
                def _():
                    y_copy(rel, s, h, False).wait_send()

                core_copy(rel, s, h).wait_send()
    for j in range(CHUNKS):
        for way in range(2):
            for h in range(HALVES):
                first_copy(way, h, j).wait_send()
            later_copy(1, way, j).wait_send()
            later_copy(2, way, j).wait_send()


def shards(eigvecs, slice_counts, occ_index, occ_levels):
    rows, depth = eigvecs.shape
    width = rows // CHUNKS
    dma = pltpu.SemaphoreType.DMA
    vmem = pl.BlockSpec(memory_space=pltpu.VMEM)
    return pl.pallas_call(
        kernel,
        out_shape=jax.ShapeDtypeStruct((2 * SUB, rows), F32),
        in_specs=[vmem, vmem, vmem, pl.BlockSpec(memory_space=pltpu.SMEM)],
        out_specs=vmem,
        scratch_shapes=[
            pltpu.VMEM((4, 2, 2, HALVES, HROWS, depth), F32),
            pltpu.VMEM((HALVES, HROWS, depth), F32),
            pltpu.VMEM((CHUNKS, width, depth), F32),
            pltpu.VMEM((4, 2, SUB, 2 * depth), BF16),
            pltpu.VMEM((4, 2, SUB, 2 * depth), BF16),
            pltpu.VMEM((rows, 2 * depth), BF16),
            pltpu.VMEM((rows, 2 * depth), BF16),
            pltpu.VMEM((3, 2, CHUNKS, SUB, width), F32),
            pltpu.VMEM((3, 2, CHUNKS, SUB, width), F32),
            dma((2, HALVES)),
            dma((2, 4, 2, HALVES)),
            dma((4, 2, HALVES)),
            dma((4, 2, 2, HALVES)),
            dma((CHUNKS,)),
            dma((CHUNKS,)),
            dma((2, HALVES, CHUNKS)),
            dma((2, HALVES, CHUNKS)),
            dma((2, 2, CHUNKS)),
            dma((2, 2, CHUNKS)),
        ],
        compiler_params=pltpu.CompilerParams(
            collective_id=0, has_side_effects=True, vmem_limit_bytes=60 * 1024 * 1024
        ),
    )(eigvecs, occ_index.reshape(1, depth), occ_levels.reshape(-1, 1), slice_counts)


def solution(mesh):
    return jax.shard_map(
        shards,
        mesh=mesh,
        in_specs=(P("row", "cuts"), P("cuts"), P("cuts"), P()),
        out_specs=P("cuts", "row"),
        check_vma=False,
    )
```

time: 329 us -> 143 us (0.43)
  waiting for transfers between devices: 281 us -> 0 us
  Pallas kernels: 0 us -> 138 us
  matrix products: 32.7 us -> 0 us
  between operations: 13.8 us -> 0.66 us
  local copies, waits for them, and re-layouts: 0.01 us -> 4.52 us
    reduce_scatter x2 -> x0, waiting for transfers between devices: 204 us -> none  [sum_by_axis(): total = lax.psum_scatter(total, axis, scatter_dimension=0, tiled=True)]
    pallas_call x0 -> x1, Pallas kernels: none -> 138 us  [shards(): pl.pallas_call(kernel, out_shape=jax.ShapeDtypeStruct((2 * SUB, rows), F3...]
    all_gather x1 -> x0, waiting for transfers between devices: 76.3 us -> none  [shards(): gathered = lax.all_gather(local_rows, 'row', axis=0, tiled=True)]
    dot_general x2 -> x0, matrix products: 32.7 us -> none  [the longest x1 31.7 us: shards(): lax.dot_general(gathered, eigvecs, (((1,), (1,)), ((), ())), precision=la...]
  transfers between devices with their start and end apart: 3 -> 0, of which waited for: 3 -> 0; matrix products, arithmetic and copies ran while one was open for 0% -> 0% of each run, Pallas kernels for 0% -> 0%
where the time goes in v1:
time: 143 us
  Pallas kernels  138 us (97%)
  local copies, waits for them, and re-layouts  4.52 us (3%)
    pallas_call x1, Pallas kernels, shards(): pl.pallas_call(kernel, out_shape=jax.ShapeDtypeStruct((2 * SUB, rows), F3...  138 us
    unnamed x1, local copies, waits for them, and re-layouts  3.16 us

profile of v1, /device:TPU:1, one launch (start us, length us, event | category | flops | bytes accessed | tf_op | source)
XLA Modules:
  0.0 142.9 jit_solution(5161747571142341652)
XLA Ops:
  0.7 1.4 copy.5.lev_ref
  2.0 137.8 %shard_map.46 = f32[512,1024]{1,0:T(8,128)} custom-call(f32[1024,512]{1,0:T(8,128)} %e_ref.1, s32[1,512]{1,0:T(1,128)} %bitcast.2, f32[64,1]{1,0:T(8,128)} %copy.5.lev_ref, s32[1]{0:T(128)S(6)} %copy.7.cnt_ref), custom_call_target="tpu_custom_call" | custom-call | tf_op jit(solution)/shard_map/pallas_call | solution.py:320
  139.8 3.2 %copy.8 = f32[512,1024]{1,0:T(8,128)} copy(f32[512,1024]{1,0:T(8,128)} %shard_map.46) | data formatting | bytes 4194304

commit v2 on v1

v2 whole, which is shorter than its diff:
```python
import jax
import jax.numpy as jnp
from jax import lax
from jax.experimental import pallas as pl
from jax.experimental.pallas import tpu as pltpu
from jax.sharding import PartitionSpec as P

MESH = pl.DeviceIdType.MESH
SUB = 256
HALVES = 2
HROWS = SUB // HALVES
CHUNKS = 4
F32, BF16 = jnp.float32, jnp.bfloat16


def split(value):
    high = value.astype(BF16)
    return high, (value - high.astype(F32)).astype(BF16)


def kernel(
    e_ref, idx_ref, lev_ref, cnt_ref, out_ref,
    p_buf, own_p, via_x, via_y, w_own, w_in, e_in, p_hi, p_lo, e_hi, e_lo, part, zin,
    w_sem, vx_sem, vy_sem, xs_sem, ys_sem, cs_sem, p_sem, es_sem, er_sem, zs_sem, zr_sem,
):
    rows, depth = e_ref.shape
    width = rows // CHUNKS
    c, r = lax.axis_index("cuts"), lax.axis_index("row")
    z, xl = c // 2, lax.rem(c, 2)
    q, core = r // 2, lax.rem(r, 2)
    xh, y = q // 4, lax.rem(q, 4)
    x = xh * 2 + xl

    def device(dx=0, dy=0, dz=0, dcore=0):
        nx, ny = lax.rem(x + dx + 4, 4), lax.rem(y + dy + 4, 4)
        nz, ncore = lax.rem(z + dz + 4, 4), lax.rem(core + dcore, 2)
        return (nz * 2 + lax.rem(nx, 2), ((nx // 2) * 4 + ny) * 2 + ncore)

    pair = (z * 2 + 1 - xl, r)
    other = device(dx=3 - 2 * xl)
    source = lax.rem(y, 2) == xl
    even_row = y // 2 == lax.rem(z, 2)
    bridge = jnp.logical_not(source)
    source_even = source & even_row
    source_odd = source & jnp.logical_not(even_row)

    def base(dy):
        return lax.rem(2 * xh + lax.rem(y + dy, 4) // 2 - z + 4, 4)

    own_rel = base(0)
    far_rel = lax.rem(own_rel + 2, 4)

    def row_gap(rel):
        return lax.rem(2 * lax.rem(z + rel, 2) + xl - y + 4, 4)

    barrier = pltpu.get_barrier_semaphore()
    for peer in (
        device(dx=1), device(dx=3), device(dy=1), device(dy=3),
        device(dz=1), device(dz=3), device(dcore=1),
    ):
        pl.semaphore_signal(barrier, inc=1, device_id=peer, device_id_type=MESH)

    level = lax.broadcasted_iota(jnp.int32, (lev_ref.shape[0], depth), 0)
    chosen = jnp.where(level == idx_ref[...], lev_ref[...], F32(0.0))
    values = jnp.sum(chosen, axis=0, keepdims=True)
    live = lax.broadcasted_iota(jnp.int32, (1, depth), 1) < cnt_ref[0]
    weights = jnp.where(live, values, F32(0.0))
    w_own[...] = jnp.broadcast_to(weights, w_own.shape)
    for h in range(HALVES):
        own_p[h] = e_ref[h * HROWS : (h + 1) * HROWS, :] * weights

    @pl.when(source)
    def _():
        for h in range(HALVES):
            p_buf[own_rel, core, 0, h] = own_p[h]

    pl.semaphore_wait(barrier, 7)

    def copy(src, dst, send, recv, peer):
        return pltpu.make_async_remote_copy(
            src_ref=src, dst_ref=dst, send_sem=send, recv_sem=recv,
            device_id=peer, device_id_type=MESH,
        )

    def w_copy():
        return copy(w_own, w_in, w_sem.at[0], w_sem.at[1], pair)

    def e_copy(i):
        return copy(
            e_ref.at[pl.ds(i * HROWS, HROWS)], e_in.at[i], es_sem.at[i], er_sem.at[i], pair
        )

    def slot_of(rel, s, h):
        return p_buf.at[rel, core, s, h], p_sem.at[rel, core, s, h]

    def to_via_x(h):
        return copy(own_p.at[h], via_x.at[h], xs_sem.at[0, h], vx_sem.at[h], other)

    def from_via_x(h):
        slot, recv = slot_of(far_rel, 0, h)
        return copy(via_x.at[h], slot, xs_sem.at[1, h], recv, pair)

    def to_source(h):
        slot, recv = slot_of(own_rel, 1, h)
        return copy(own_p.at[h], slot, xs_sem.at[0, h], recv, other)

    def to_via_y(side, h):
        return copy(
            own_p.at[h], via_y.at[side, h], xs_sem.at[2 + side, h], vy_sem.at[side, h],
            device(dy=3 if side == 0 else 1),
        )

    def from_via_y(side, h):
        slot, recv = slot_of(base(1 if side == 0 else 3), 1, h)
        return copy(via_y.at[side, h], slot, xs_sem.at[2 + side, h], recv, other)

    def y_copy(rel, s, h, up):
        slot, recv = slot_of(rel, s, h)
        return copy(
            slot, slot, ys_sem.at[0 if up else 1, rel, s, h], recv, device(dy=1 if up else 3)
        )

    def core_copy(rel, s, h):
        slot, recv = slot_of(rel, s, h)
        return copy(slot, slot, cs_sem.at[rel, s, h], recv, device(dcore=1))

    def landed(ref, sem):
        pltpu.make_async_copy(ref, ref, sem).wait()

    def arrive(rel, k, s, h):
        landed(p_buf.at[rel, k, s, h], p_sem.at[rel, k, s, h])

    def keep(rel, k, s, h):
        high, low = split(p_buf[rel, k, s, h])
        rows_of = pl.ds(h * HROWS, HROWS)
        p_hi[rel, k, rows_of, s * depth : (s + 1) * depth] = high
        p_lo[rel, k, rows_of, s * depth : (s + 1) * depth] = low

    def sends(rel, s, up):
        gap = row_gap(rel)
        first_hop = gap == 0
        if s == 1:
            first_hop = first_hop & (rel != far_rel)
        if up and s == 0:
            return first_hop | (gap == 3)
        if not up and s == 1:
            return first_hop | (gap == 1)
        return first_hop

    def hand_on(rel, s, h):
        for up in (True, False):
            pl.when(sends(rel, s, up))(lambda up=up: y_copy(rel, s, h, up).start())
        core_copy(rel, s, h).start()
        keep(rel, core, s, h)

    def take(rel, s, h):
        arrive(rel, core, s, h)
        hand_on(rel, s, h)

    def weigh(h):
        landed(e_in.at[h], er_sem.at[h])
        p_buf[own_rel, core, 1, h] = e_in[h] * w_in[0:1, :]
        hand_on(own_rel, 1, h)

    def need(rel, h):
        for s in range(2):
            arrive(rel, 1 - core, s, h)
            keep(rel, 1 - core, s, h)

    def take_far(h):
        far = base(2)
        far_next = lax.rem(far + 2, 4)
        take(far, 0, h)
        take(far, 1, h)
        take(far_next, 0, h)
        take(far_next, 1, h)

    def take_sides(h):
        up, down = base(1), base(3)
        up_next, down_next = lax.rem(up + 2, 4), lax.rem(down + 2, 4)
        take(up, 0, h)
        take(down, 0, h)
        take(up, 1, h)
        take(down, 1, h)
        take(up_next, 0, h)
        take(down_next, 0, h)
        take(up_next, 1, h)
        take(down_next, 1, h)

    def begin_source():
        to_via_x(0).start()
        w_copy().start()
        for i in range(2 * CHUNKS):
            e_copy(i).start()
        hand_on(own_rel, 0, 0)
        landed(w_in, w_sem.at[1])
        weigh(0)
        for side in range(2):
            landed(via_y.at[side, 0], vy_sem.at[side, 0])
            from_via_y(side, 0).start()
        to_via_x(1).start()
        take(far_rel, 1, 0)
        take(far_rel, 0, 0)
        hand_on(own_rel, 0, 1)
        for side in range(2):
            landed(via_y.at[side, 1], vy_sem.at[side, 1])
            from_via_y(side, 1).start()
        take(far_rel, 1, 1)
        weigh(1)

    def begin_bridge():
        for h in range(HALVES):
            to_source(h).start()
            for side in range(2):
                to_via_y(side, h).start()
        w_copy().start()
        e_copy(0).start()
        landed(w_in, w_sem.at[1])
        landed(via_x.at[0], vx_sem.at[0])
        from_via_x(0).start()
        e_copy(1).start()
        e_copy(2).start()
        take_sides(0)
        landed(via_x.at[1], vx_sem.at[1])
        from_via_x(1).start()
        for i in range(3, 2 * CHUNKS):
            e_copy(i).start()
        for i in range(2):
            landed(e_in.at[i], er_sem.at[i])

    def split_rows(j):
        span = pl.ds(j * width, width)
        high, low = split(e_ref[span, :])
        e_hi[span, :depth] = high
        e_lo[span, :depth] = low

    def get_rows(j):
        for i in range(2):
            if j > 0:
                landed(e_in.at[2 * j + i], er_sem.at[2 * j + i])
            span = pl.ds(j * width + i * HROWS, HROWS)
            high, low = split(e_in[2 * j + i])
            e_hi[span, depth:] = high
            e_lo[span, depth:] = low

    def dot(a, b):
        return lax.dot_general(a, b, (((1,), (1,)), ((), ())), preferred_element_type=F32)

    def tile(rel, k, rows_of, j):
        span = pl.ds(j * width, width)
        high, low = p_hi[rel, k, rows_of, :], p_lo[rel, k, rows_of, :]
        e_high, e_low = e_hi[span, :], e_lo[span, :]
        return dot(high, e_high) + (dot(high, e_low) + dot(low, e_high))

    def z_copy(kind, way, h, j):
        rows_of = pl.ds(h * HROWS, HROWS)
        nz = lax.rem(z + 1 + 2 * way, 4)
        return copy(
            part.at[kind, way, j, rows_of], zin.at[kind, way, j, rows_of],
            zs_sem.at[kind, way, h, j], zr_sem.at[kind, way, h, j], (nz * 2 + xl, r),
        )

    def z_landed(kind, way, h, j):
        landed(zin.at[kind, way, j, pl.ds(h * HROWS, HROWS)], zr_sem.at[kind, way, h, j])

    def stage(kind, halves, j):
        rows_of = pl.ds(halves[0] * HROWS, len(halves) * HROWS)

        def step(way, carry):
            if kind == 0:
                total = tile(2, way, rows_of, j)
            elif kind == 1:
                total = tile(1 + 2 * way, 1 - way, rows_of, j)
            else:
                total = tile(1 + 2 * way, way, rows_of, j)
                for h in halves:
                    z_landed(0, way, h, j)
                total = total + zin[0, way, j, rows_of]
            part[kind, way, j, rows_of] = total
            for h in halves:
                z_copy(kind, way, h, j).start()
            return carry

        lax.fori_loop(0, 2, step, 0)

    def first(halves, j):
        stage(0, halves, j)

    def second(halves, j):
        stage(1, halves, j)

    def third(halves, j):
        stage(2, halves, j)

    def last(j):
        def step(k, carry):
            rows_of = pl.ds(k * SUB, SUB)
            out_ref[rows_of, j * width : (j + 1) * width] = tile(0, k, pl.ds(0, SUB), j)
            return carry

        lax.fori_loop(0, 2, step, 0)

    def finish(j):
        def step(k, carry):
            rows_of = pl.ds(k * SUB, SUB)
            for h in range(HALVES):
                z_landed(1, 1 - k, h, j)
                z_landed(2, k, h, j)
            out_ref[rows_of, j * width : (j + 1) * width] += zin[2, k, j] + zin[1, 1 - k, j]
            return carry

        lax.fori_loop(0, 2, step, 0)

    def begin():
        pl.when(source)(begin_source)
        pl.when(bridge)(begin_bridge)

    def some_first():
        @pl.when(source_even)
        def _():
            need(2, 0)
            first((0,), 0)

        @pl.when(source_odd)
        def _():
            need(1, 0)
            need(3, 0)
            second((0,), 0)

    def other_first():
        @pl.when(source)
        def _():
            take_far(0)

        @pl.when(jnp.logical_not(source_even))
        def _():
            need(2, 0)
            first((0,), 0)

        @pl.when(jnp.logical_not(source_odd))
        def _():
            need(1, 0)
            need(3, 0)
            second((0,), 0)

    def row_rest():
        @pl.when(source)
        def _():
            take(far_rel, 0, 1)

    def side_rest():
        pl.when(source)(lambda: take_far(1))
        pl.when(bridge)(lambda: take_sides(1))
        for rel in (2, 1, 3):
            need(rel, 1)

    for j in range(CHUNKS):
        split_rows(j)
    begin()
    get_rows(0)
    some_first()
    other_first()
    row_rest()
    third((0,), 0)
    get_rows(1)
    first((0,), 1)
    second((0,), 1)
    third((0,), 1)
    side_rest()
    first((1,), 0)
    second((1,), 0)
    third((1,), 0)
    first((1,), 1)
    second((1,), 1)
    third((1,), 1)
    get_rows(2)
    first((0, 1), 2)
    second((0, 1), 2)
    third((0, 1), 2)
    get_rows(3)
    first((0, 1), 3)
    second((0, 1), 3)
    third((0, 1), 3)
    need(0, 0)
    need(0, 1)
    for j in range(CHUNKS):
        last(j)
    for j in range(CHUNKS):
        finish(j)

    w_copy().wait_send()
    for i in range(2 * CHUNKS):
        e_copy(i).wait_send()
    for h in range(HALVES):
        for lane in range(4):
            if lane == 1:
                pl.when(bridge)(lambda: from_via_x(h).wait_send())
            elif lane == 0:
                to_via_x(h).wait_send()
            else:
                to_via_y(lane - 2, h).wait_send()
    for rel in range(4):
        for s in range(2):
            for h in range(HALVES):
                for up in (True, False):
                    pl.when(sends(rel, s, up))(lambda up=up: y_copy(rel, s, h, up).wait_send())
                core_copy(rel, s, h).wait_send()
    for kind in range(3):
        for way in range(2):
            for h in range(HALVES):
                for j in range(CHUNKS):
                    z_copy(kind, way, h, j).wait_send()


def shards(eigvecs, slice_counts, occ_index, occ_levels):
    rows, depth = eigvecs.shape
    width = rows // CHUNKS
    dma = pltpu.SemaphoreType.DMA
    vmem = pl.BlockSpec(memory_space=pltpu.VMEM)
    return pl.pallas_call(
        kernel,
        out_shape=jax.ShapeDtypeStruct((2 * SUB, rows), F32),
        in_specs=[vmem, vmem, vmem, pl.BlockSpec(memory_space=pltpu.SMEM)],
        out_specs=vmem,
        scratch_shapes=[
            pltpu.VMEM((4, 2, 2, HALVES, HROWS, depth), F32),
            pltpu.VMEM((HALVES, HROWS, depth), F32),
            pltpu.VMEM((HALVES, HROWS, depth), F32),
            pltpu.VMEM((2, HALVES, HROWS, depth), F32),
            pltpu.VMEM((8, depth), F32),
            pltpu.VMEM((8, depth), F32),
            pltpu.VMEM((2 * CHUNKS, HROWS, depth), F32),
            pltpu.VMEM((4, 2, SUB, 2 * depth), BF16),
            pltpu.VMEM((4, 2, SUB, 2 * depth), BF16),
            pltpu.VMEM((rows, 2 * depth), BF16),
            pltpu.VMEM((rows, 2 * depth), BF16),
            pltpu.VMEM((3, 2, CHUNKS, SUB, width), F32),
            pltpu.VMEM((3, 2, CHUNKS, SUB, width), F32),
            dma((2,)),
            dma((HALVES,)),
            dma((2, HALVES)),
            dma((4, HALVES)),
            dma((2, 4, 2, HALVES)),
            dma((4, 2, HALVES)),
            dma((4, 2, 2, HALVES)),
            dma((2 * CHUNKS,)),
            dma((2 * CHUNKS,)),
            dma((3, 2, HALVES, CHUNKS)),
            dma((3, 2, HALVES, CHUNKS)),
        ],
        compiler_params=pltpu.CompilerParams(
            collective_id=0, has_side_effects=True, vmem_limit_bytes=60 * 1024 * 1024
        ),
    )(eigvecs, occ_index.reshape(1, depth), occ_levels.reshape(-1, 1), slice_counts)


def solution(mesh):
    return jax.shard_map(
        shards,
        mesh=mesh,
        in_specs=(P("row", "cuts"), P("cuts"), P("cuts"), P()),
        out_specs=P("cuts", "row"),
        check_vma=False,
    )
```

time: 143 us -> 125 us (0.87)
  Pallas kernels: 138 us -> 119 us
    pallas_call x1, Pallas kernels: 138 us -> 119 us  [shards(): pl.pallas_call(kernel, out_shape=jax.ShapeDtypeStruct((2 * SUB, rows), F3...]
where the time goes in v2:
time: 125 us
  Pallas kernels  119 us (95%)
  local copies, waits for them, and re-layouts  4.52 us (4%)
    pallas_call x1, Pallas kernels, shards(): pl.pallas_call(kernel, out_shape=jax.ShapeDtypeStruct((2 * SUB, rows), F3...  119 us
    unnamed x1, local copies, waits for them, and re-layouts  3.16 us

profile of v2, /device:TPU:1, one launch (start us, length us, event | category | flops | bytes accessed | tf_op | source)
XLA Modules:
  0.0 124.7 jit_solution(10097702436689583140)
XLA Ops:
  0.7 1.4 %copy.5.lev_ref = f32[64,1]{1,0:T(8,128)} copy(f32[64,1]{0,1:T(1,128)} %bitcast.3) | data formatting | bytes 512 | tf_op jit(solution)/shard_map/reshape | solution.py:454
  2.0 119.5 %shard_map.46 = f32[512,1024]{1,0:T(8,128)} custom-call(f32[1024,512]{1,0:T(8,128)} %e_ref.1, s32[1,512]{1,0:T(1,128)} %bitcast.2, f32[64,1]{1,0:T(8,128)} %copy.5.lev_ref, s32[1]{0:T(128)S(6)} %copy.7.cnt_ref), custom_call_target="tpu_custom_call" | custom-call | tf_op jit(solution)/shard_map/pallas_call | solution.py:420
  121.5 3.2 %copy.8 = f32[512,1024]{1,0:T(8,128)} copy(f32[512,1024]{1,0:T(8,128)} %shard_map.46) | data formatting | bytes 4194304

commit v3 on v0

v3 whole, which is shorter than its diff:
```python
import jax
import jax.numpy as jnp
from jax import lax
from jax.experimental import pallas as pl
from jax.experimental.pallas import tpu as pltpu
from jax.sharding import PartitionSpec as P

MESH = pl.DeviceIdType.MESH
SUB = 256
PIECES = 4
PROWS = SUB // PIECES
CHUNKS = 4
F32, BF16 = jnp.float32, jnp.bfloat16


def split(value):
    high = value.astype(BF16)
    return high, (value - high.astype(F32)).astype(BF16)


def kernel(
    e_any, idx_any, lev_any, cnt_any, out_ref,
    e_ref, idx_ref, lev_ref, cnt_ref, in_sem, p_buf, own_p, via_x, via_y, w_own, w_in, e_in, p_hi, p_lo, e_hi, e_lo, part, zin,
    w_sem, vx_sem, vy_sem, xs_sem, ys_sem, cs_sem, p_sem, es_sem, er_sem, zs_sem, zr_sem,
):
    rows, depth = e_ref.shape
    width = rows // CHUNKS
    c, r = lax.axis_index("cuts"), lax.axis_index("row")
    z, xl = c // 2, lax.rem(c, 2)
    q, core = r // 2, lax.rem(r, 2)
    xh, y = q // 4, lax.rem(q, 4)
    x = xh * 2 + xl

    def device(dx=0, dy=0, dz=0, dcore=0):
        nx, ny = lax.rem(x + dx + 4, 4), lax.rem(y + dy + 4, 4)
        nz, ncore = lax.rem(z + dz + 4, 4), lax.rem(core + dcore, 2)
        return (nz * 2 + lax.rem(nx, 2), ((nx // 2) * 4 + ny) * 2 + ncore)

    pair = (z * 2 + 1 - xl, r)
    other = device(dx=3 - 2 * xl)
    source = lax.rem(y, 2) == xl
    even_row = y // 2 == lax.rem(z, 2)
    bridge = jnp.logical_not(source)
    source_odd = source & jnp.logical_not(even_row)

    near_odd = jnp.where(source_odd, 1, 0)
    far_odd = 1 - near_odd

    def base(dy):
        return lax.rem(2 * xh + lax.rem(y + dy, 4) // 2 - z + 4, 4)

    own_rel = base(0)
    far_rel = lax.rem(own_rel + 2, 4)

    def row_gap(rel):
        return lax.rem(2 * lax.rem(z + rel, 2) + xl - y + 4, 4)

    barrier = pltpu.get_barrier_semaphore()
    for peer in (
        device(dx=1), device(dx=3), device(dy=1), device(dy=3),
        device(dz=1), device(dz=3), device(dcore=1),
    ):
        pl.semaphore_signal(barrier, inc=1, device_id=peer, device_id_type=MESH)

    picked, others = pl.ds(0, SUB), pl.ds(SUB, rows - SUB)
    small = [
        pltpu.make_async_copy(src, dst, in_sem.at[n])
        for n, (src, dst) in enumerate(
            ((idx_any, idx_ref), (lev_any, lev_ref), (cnt_any, cnt_ref))
        )
    ]
    load_picked = pltpu.make_async_copy(e_any.at[picked], e_ref.at[picked], in_sem.at[3])
    load_others = pltpu.make_async_copy(e_any.at[others], e_ref.at[others], in_sem.at[4])
    for load in (*small, load_picked, load_others):
        load.start()
    for load in small:
        load.wait()
    count = lev_ref.shape[1]
    diagonal = lax.broadcasted_iota(jnp.int32, (count, count), 0) == lax.broadcasted_iota(
        jnp.int32, (count, count), 1
    )
    levels = jnp.sum(jnp.where(diagonal, lev_ref[...], F32(0.0)), axis=1, keepdims=True)
    level = lax.broadcasted_iota(jnp.int32, (count, depth), 0)
    chosen = jnp.where(level == idx_ref[...], levels, F32(0.0))
    values = jnp.sum(chosen, axis=0, keepdims=True)
    live = lax.broadcasted_iota(jnp.int32, (1, depth), 1) < cnt_ref[...]
    weights = jnp.where(live, values, F32(0.0))
    w_own[...] = jnp.broadcast_to(weights, w_own.shape)
    load_picked.wait()
    for h in range(PIECES):
        own_p[h] = e_ref[h * PROWS : (h + 1) * PROWS, :] * weights

    @pl.when(source)
    def _():
        for h in range(PIECES):
            p_buf[own_rel, core, 0, h] = own_p[h]

    load_others.wait()
    pl.semaphore_wait(barrier, 7)

    def copy(src, dst, send, recv, peer):
        return pltpu.make_async_remote_copy(
            src_ref=src, dst_ref=dst, send_sem=send, recv_sem=recv,
            device_id=peer, device_id_type=MESH,
        )

    def w_copy():
        return copy(w_own, w_in, w_sem.at[0], w_sem.at[1], pair)

    def e_copy(i):
        return copy(e_ref.at[pl.ds(i * PROWS, PROWS)], e_in.at[i], es_sem, er_sem.at[i], pair)

    def slot_of(rel, s, h):
        return p_buf.at[rel, core, s, h], p_sem.at[rel, core, s, h]

    def to_via_x(h):
        return copy(own_p.at[h], via_x.at[h], xs_sem, vx_sem.at[h], other if h % 2 == 0 else pair)

    def from_via_x(h):
        slot, recv = slot_of(far_rel if h % 2 == 0 else own_rel, 0, h)
        return copy(via_x.at[h], slot, xs_sem, recv, pair if h % 2 == 0 else other)

    def to_source(h):
        slot, recv = slot_of(own_rel, 1, h)
        return copy(own_p.at[h], slot, xs_sem, recv, other)

    def to_via_y(side, h):
        return copy(
            own_p.at[h], via_y.at[side, h], xs_sem, vy_sem.at[side, h],
            device(dy=3 if side == 0 else 1),
        )

    def from_via_y(side, h):
        slot, recv = slot_of(base(1 if side == 0 else 3), 1, h)
        return copy(via_y.at[side, h], slot, xs_sem, recv, other)

    def y_copy(rel, s, h, up):
        slot, recv = slot_of(rel, s, h)
        return copy(slot, slot, ys_sem, recv, device(dy=1 if up else 3))

    def core_copy(rel, s, h):
        slot, recv = slot_of(rel, s, h)
        return copy(slot, slot, cs_sem, recv, device(dcore=1))

    def landed(ref, sem):
        pltpu.make_async_copy(ref, ref, sem).wait()

    def arrive(rel, k, s, h):
        landed(p_buf.at[rel, k, s, h], p_sem.at[rel, k, s, h])

    def spot(rel, k):
        return lax.rem(rel, 2), pl.ds(pl.multiple_of((rel // 2) * 2 * PROWS + k * PROWS, PROWS), PROWS)

    def keep(rel, k, s, h):
        high, low = split(p_buf[rel, k, s, h])
        odd, rows_of = spot(rel, k)
        p_hi[h, odd, rows_of, s * depth : (s + 1) * depth] = high
        p_lo[h, odd, rows_of, s * depth : (s + 1) * depth] = low

    def sends(rel, s, up):
        gap = row_gap(rel)
        first_hop = gap == 0
        if s == 1:
            first_hop = first_hop & (rel != far_rel)
        if up and s == 0:
            return first_hop | (gap == 3)
        if not up and s == 1:
            return first_hop | (gap == 1)
        return first_hop

    def hand_on(rel, s, h):
        for up in (True, False):
            pl.when(sends(rel, s, up))(lambda up=up: y_copy(rel, s, h, up).start())
        core_copy(rel, s, h).start()
        keep(rel, core, s, h)

    def take(rel, s, h):
        arrive(rel, core, s, h)
        hand_on(rel, s, h)

    def weigh(h):
        landed(e_in.at[h], er_sem.at[h])
        p_buf[own_rel, core, 1, h] = e_in[h] * w_in[0:1, :]
        hand_on(own_rel, 1, h)

    def need(odd, h):
        for step in range(2):
            for s in range(2):
                arrive(odd + 2 * step, 1 - core, s, h)
                keep(odd + 2 * step, 1 - core, s, h)

    def relay_x(h):
        landed(via_x.at[h], vx_sem.at[h])
        from_via_x(h).start()

    def relay_y(h):
        for side in range(2):
            landed(via_y.at[side, h], vy_sem.at[side, h])
            from_via_y(side, h).start()

    def send_rows(start, stop):
        for i in range(start, stop):
            e_copy(i).start()

    def take_far(h):
        far = base(2)
        far_next = lax.rem(far + 2, 4)
        take(far, 0, h)
        take(far, 1, h)
        take(far_next, 1, h)
        take(far_next, 0, h)

    def take_sides(h, part):
        up, down = base(1), base(3)
        up_next, down_next = lax.rem(up + 2, 4), lax.rem(down + 2, 4)
        if part == 0:
            take(up, 0, h)
            take(down, 0, h)
            take(up, 1, h)
            take(down, 1, h)
        else:
            take(up_next, 1, h)
            take(down_next, 1, h)
            take(up_next, 0, h)
            take(down_next, 0, h)

    def begin_source():
        to_via_x(0).start()
        w_copy().start()
        send_rows(0, 1)
        to_via_x(1).start()
        send_rows(1, 6)
        to_via_x(3).start()
        send_rows(6, 16)
        hand_on(own_rel, 0, 0)
        landed(w_in, w_sem.at[1])
        weigh(0)
        relay_y(0)
        to_via_x(2).start()
        take(far_rel, 1, 0)
        hand_on(own_rel, 0, 1)
        take(far_rel, 0, 0)
        weigh(1)
        relay_y(1)
        take(far_rel, 1, 1)
        take(far_rel, 0, 1)
        hand_on(own_rel, 0, 2)
        weigh(2)
        take(far_rel, 1, 2)
        relay_y(2)
        relay_y(3)
        hand_on(own_rel, 0, 3)
        weigh(3)
        take(far_rel, 1, 3)
        get_rows(0)
        near_part(0)
        near_part(1)
        take_far(0)
        need(far_odd, 0)
        half(far_odd, 0, 0)
        take(far_rel, 0, 2)
        near_part(2)
        take(far_rel, 0, 3)
        near_part(3)

    def near_part(h):
        need(near_odd, h)
        half(near_odd, h, 0)

    def begin_bridge():
        for h in range(2):
            to_source(h).start()
        for h in range(PIECES):
            for side in range(2):
                to_via_y(side, h).start()
        w_copy().start()
        send_rows(0, 1)
        relay_x(0)
        send_rows(1, 4)
        relay_x(1)
        for h in range(2, PIECES):
            to_source(h).start()
        take_sides(0, 0)
        take_sides(0, 1)
        relay_x(2)
        send_rows(4, 16)
        landed(w_in, w_sem.at[1])
        for i in range(4):
            landed(e_in.at[i], er_sem.at[i])
        get_rows(0)
        for odd in range(2):
            need(odd, 0)
            half(odd, 0, 0)
        take_sides(1, 0)
        take_sides(1, 1)
        relay_x(3)

    def split_rows(j):
        span = pl.ds(j * width, width)
        high, low = split(e_ref[span, :])
        e_hi[span, :depth] = high
        e_lo[span, :depth] = low

    def get_rows(j):
        for i in range(4 * j, 4 * j + 4):
            if j > 0:
                landed(e_in.at[i], er_sem.at[i])
            span = pl.ds(i * PROWS, PROWS)
            high, low = split(e_in[i])
            e_hi[span, depth:] = high
            e_lo[span, depth:] = low

    def dot(a, b):
        return lax.dot_general(a, b, (((1,), (1,)), ((), ())), preferred_element_type=F32)

    def z_copy(kind, way, h, j):
        rel = jnp.where(kind == 0, 2, 1 + 2 * way)
        k = jnp.where(kind == 1, 1 - way, way)
        nz = lax.rem(z + 1 + 2 * way, 4)
        odd, rows_of = spot(rel, k)
        return copy(
            part.at[h, j, odd, rows_of], zin.at[kind, way, h, j],
            zs_sem, zr_sem.at[kind, way, h, j], (nz * 2 + xl, r),
        )

    def z_landed(kind, way, h, j):
        landed(zin.at[kind, way, h, j], zr_sem.at[kind, way, h, j])

    def half(odd, h, j):
        span = pl.ds(j * width, width)
        part[h, j, odd] = dot(p_hi[h, odd], e_hi[span, :])
        part[h, j, odd] += dot(p_hi[h, odd], e_lo[span, :])
        part[h, j, odd] += dot(p_lo[h, odd], e_hi[span, :])
        for way in range(2):
            z_copy(odd, way, h, j).start()

    def both(h, j):
        half(near_odd, h, j)
        half(far_odd, h, j)

    def pass_on(h, j):
        for way in range(2):
            z_landed(0, way, h, j)
            odd, rows_of = spot(1 + 2 * way, way)
            part[h, j, odd, rows_of] += zin[0, way, h, j]
            z_copy(2, way, h, j).start()

    def finish(h, j):
        for k in range(2):
            z_landed(1, 1 - k, h, j)
            z_landed(2, k, h, j)
            odd, rows_of = spot(0, k)
            total = part[h, j, odd, rows_of] + (zin[2, k, h, j] + zin[1, 1 - k, h, j])
            out_ref[k * SUB + h * PROWS : k * SUB + (h + 1) * PROWS, j * width : (j + 1) * width] = total

    def begin():
        pl.when(source)(begin_source)
        pl.when(bridge)(begin_bridge)

    def rest(h):
        @pl.when(source)
        def _():
            take_far(h)

        @pl.when(bridge)
        def _():
            if h > 1:
                take_sides(h, 0)
                take_sides(h, 1)
            need(0, h)

        need(far_odd, h)

    def near(h, j):
        pl.when(bridge)(lambda: half(near_odd, h, j))

    def ready(h, j):
        pl.when(source)(lambda: half(near_odd, h, j))

    def far(h, j):
        half(far_odd, h, j)

    for j in range(CHUNKS):
        split_rows(j)
    begin()
    rest(1)
    near(1, 0)
    far(1, 0)
    pass_on(0, 0)
    get_rows(1)
    both(0, 1)
    pass_on(1, 0)
    both(1, 1)
    pass_on(0, 1)
    ready(2, 1)
    ready(3, 1)
    rest(2)
    near(2, 0)
    far(2, 0)
    pass_on(1, 1)
    near(2, 1)
    far(2, 1)
    pass_on(2, 0)
    get_rows(2)
    both(0, 2)
    pass_on(2, 1)
    both(1, 2)
    pass_on(0, 2)
    rest(3)
    near(3, 0)
    far(3, 0)
    pass_on(1, 2)
    near(3, 1)
    far(3, 1)
    pass_on(3, 0)
    both(2, 2)
    pass_on(3, 1)
    both(3, 2)
    pass_on(2, 2)
    get_rows(3)
    both(0, 3)
    pass_on(3, 2)
    both(1, 3)
    pass_on(0, 3)
    both(2, 3)
    pass_on(1, 3)
    both(3, 3)
    pass_on(2, 3)
    for j in range(CHUNKS - 1):
        for h in range(PIECES):
            finish(h, j)
    pass_on(3, 3)
    for h in range(PIECES):
        finish(h, CHUNKS - 1)

    w_copy().wait_send()
    landed(e_ref, es_sem)
    landed(p_buf.at[pl.ds(0, 2)], cs_sem)
    landed(zin, zs_sem)

    @pl.when(source)
    def _():
        landed(p_buf.at[pl.ds(0, 3), 0, 0], xs_sem)
        landed(p_buf.at[pl.ds(0, 3), 0], ys_sem)

    @pl.when(bridge)
    def _():
        landed(p_buf.at[0], xs_sem)
        landed(p_buf.at[0], ys_sem)


def shards(eigvecs, slice_counts, occ_index, occ_levels):
    rows, depth = eigvecs.shape
    width = rows // CHUNKS
    dma = pltpu.SemaphoreType.DMA
    levels = occ_levels.shape[0]
    return pl.pallas_call(
        kernel,
        out_shape=pltpu.VMEM((2 * SUB, rows), F32),
        in_specs=[pl.BlockSpec(memory_space=pl.ANY)] * 4,
        out_specs=pl.BlockSpec(memory_space=pltpu.VMEM),
        scratch_shapes=[
            pltpu.VMEM((rows, depth), F32),
            pltpu.VMEM((1, depth), jnp.int32),
            pltpu.VMEM((1, levels), F32),
            pltpu.VMEM((1, 1), jnp.int32),
            dma((5,)),
            pltpu.VMEM((4, 2, 2, PIECES, PROWS, depth), F32),
            pltpu.VMEM((PIECES, PROWS, depth), F32),
            pltpu.VMEM((PIECES, PROWS, depth), F32),
            pltpu.VMEM((2, PIECES, PROWS, depth), F32),
            pltpu.VMEM((8, depth), F32),
            pltpu.VMEM((8, depth), F32),
            pltpu.VMEM((rows // PROWS, PROWS, depth), F32),
            pltpu.VMEM((PIECES, 2, 4 * PROWS, 2 * depth), BF16),
            pltpu.VMEM((PIECES, 2, 4 * PROWS, 2 * depth), BF16),
            pltpu.VMEM((rows, 2 * depth), BF16),
            pltpu.VMEM((rows, 2 * depth), BF16),
            pltpu.VMEM((PIECES, CHUNKS, 2, 4 * PROWS, width), F32),
            pltpu.VMEM((3, 2, PIECES, CHUNKS, PROWS, width), F32),
            dma((2,)),
            dma((PIECES,)),
            dma((2, PIECES)),
            dma,
            dma,
            dma,
            dma((4, 2, 2, PIECES)),
            dma,
            dma((rows // PROWS,)),
            dma,
            dma((3, 2, PIECES, CHUNKS)),
        ],
        compiler_params=pltpu.CompilerParams(
            collective_id=0, has_side_effects=True, vmem_limit_bytes=60 * 1024 * 1024
        ),
    )(
        eigvecs,
        occ_index.reshape(1, depth),
        occ_levels.reshape(1, levels),
        slice_counts.reshape(1, 1),
    )


def solution(mesh):
    return jax.shard_map(
        shards,
        mesh=mesh,
        in_specs=(P("row", "cuts"), P("cuts"), P("cuts"), P()),
        out_specs=P("cuts", "row"),
        check_vma=False,
    )
```

time: 329 us -> 108 us (0.33)
  waiting for transfers between devices: 281 us -> 0 us
  Pallas kernels: 0 us -> 106 us
  matrix products: 32.7 us -> 0 us
  between operations: 13.8 us -> 0.66 us
    reduce_scatter x2 -> x0, waiting for transfers between devices: 204 us -> none  [sum_by_axis(): total = lax.psum_scatter(total, axis, scatter_dimension=0, tiled=True)]
    pallas_call x0 -> x1, Pallas kernels: none -> 106 us  [shards(): pl.pallas_call(kernel, out_shape=pltpu.VMEM((2 * SUB, rows), F32), in_spe...]
    all_gather x1 -> x0, waiting for transfers between devices: 76.3 us -> none  [shards(): gathered = lax.all_gather(local_rows, 'row', axis=0, tiled=True)]
    dot_general x2 -> x0, matrix products: 32.7 us -> none  [the longest x1 31.7 us: shards(): lax.dot_general(gathered, eigvecs, (((1,), (1,)), ((), ())), precision=la...]
  transfers between devices with their start and end apart: 3 -> 0, of which waited for: 3 -> 0; matrix products, arithmetic and copies ran while one was open for 0% -> 0% of each run, Pallas kernels for 0% -> 0%
where the time goes in v3:
time: 108 us
  Pallas kernels  106 us (98%)
  local copies, waits for them, and re-layouts  1.32 us (1%)
    pallas_call x1, Pallas kernels, shards(): pl.pallas_call(kernel, out_shape=pltpu.VMEM((2 * SUB, rows), F32), in_spe...  106 us

profile of v3, /device:TPU:1, one launch (start us, length us, event | category | flops | bytes accessed | tf_op | source)
XLA Modules:
  0.0 108.2 jit_solution(11010732503645381181)
XLA Ops:
  0.7 106.2 %shard_map.46 = f32[512,1024]{1,0:T(8,128)S(1)} custom-call(f32[1024,512]{1,0:T(8,128)} %e_any.1, s32[1,512]{1,0:T(1,128)} %bitcast.4, f32[1,64]{1,0:T(1,128)} %bitcast.5, s32[1,1]{1,0:T(1,128)} %bitcast.3.cnt_any), custom_call_target="tpu_custom_call" | custom-call | tf_op jit(solution)/shard_map/pallas_call | solution.py:457
  106.8 1.3 %copy.6 = f32[512,1024]{1,0:T(8,128)} copy(f32[512,1024]{1,0:T(8,128)S(1)} %shard_map.46) | data formatting | bytes 4194304

commit v4 on v3

v4 whole, which is shorter than its diff:
```python
import jax
import jax.numpy as jnp
from jax import lax
from jax.experimental import pallas as pl
from jax.experimental.pallas import tpu as pltpu
from jax.sharding import PartitionSpec as P

MESH = pl.DeviceIdType.MESH
SUB = 256
PIECES = 4
PROWS = SUB // PIECES
WIDE = 128
FIRST, SECOND, THIRD, FOURTH = (0, 2), (2, 2), (4, 2), (6, 2)
SECOND_A, SECOND_B = (2, 1), (3, 1)
F32, BF16 = jnp.float32, jnp.bfloat16


def split(value):
    high = value.astype(BF16)
    return high, (value - high.astype(F32)).astype(BF16)


def kernel(
    e_any, idx_any, lev_any, cnt_any, out_ref,
    e_ref, idx_ref, lev_ref, cnt_ref, in_sem, p_buf, own_p, via_x, via_y, w_own, w_in, e_in, p_hi, p_lo, e_hi, e_lo, part, first_in, second_in, third_in,
    w_sem, vx_sem, vy_sem, xs_sem, ys_sem, cs_sem, p_sem, es_sem, er_sem, zs_sem, first_sem, later_sem,
):
    rows, depth = e_ref.shape
    c, r = lax.axis_index("cuts"), lax.axis_index("row")
    z, xl = c // 2, lax.rem(c, 2)
    q, core = r // 2, lax.rem(r, 2)
    xh, y = q // 4, lax.rem(q, 4)
    x = xh * 2 + xl

    def device(dx=0, dy=0, dz=0, dcore=0):
        nx, ny = lax.rem(x + dx + 4, 4), lax.rem(y + dy + 4, 4)
        nz, ncore = lax.rem(z + dz + 4, 4), lax.rem(core + dcore, 2)
        return (nz * 2 + lax.rem(nx, 2), ((nx // 2) * 4 + ny) * 2 + ncore)

    pair = (z * 2 + 1 - xl, r)
    other = device(dx=3 - 2 * xl)
    source = lax.rem(y, 2) == xl
    even_row = y // 2 == lax.rem(z, 2)
    bridge = jnp.logical_not(source)
    source_odd = source & jnp.logical_not(even_row)

    source_even = source & even_row
    not_odd = jnp.logical_not(source_odd)

    def base(dy):
        return lax.rem(2 * xh + lax.rem(y + dy, 4) // 2 - z + 4, 4)

    own_rel = base(0)
    far_rel = lax.rem(own_rel + 2, 4)

    def row_gap(rel):
        return lax.rem(2 * lax.rem(z + rel, 2) + xl - y + 4, 4)

    barrier = pltpu.get_barrier_semaphore()
    for peer in (
        device(dx=1), device(dx=2), device(dx=3), device(dy=1), device(dy=3),
        device(dz=1), device(dz=3), device(dcore=1),
    ):
        pl.semaphore_signal(barrier, inc=1, device_id=peer, device_id_type=MESH)

    picked, others = pl.ds(0, SUB), pl.ds(SUB, rows - SUB)
    small = [
        pltpu.make_async_copy(src, dst, in_sem.at[n])
        for n, (src, dst) in enumerate(
            ((idx_any, idx_ref), (lev_any, lev_ref), (cnt_any, cnt_ref))
        )
    ]
    load_picked = pltpu.make_async_copy(e_any.at[picked], e_ref.at[picked], in_sem.at[3])
    load_others = pltpu.make_async_copy(e_any.at[others], e_ref.at[others], in_sem.at[4])
    for load in (*small, load_picked, load_others):
        load.start()
    for load in small:
        load.wait()
    count = lev_ref.shape[1]
    diagonal = lax.broadcasted_iota(jnp.int32, (count, count), 0) == lax.broadcasted_iota(
        jnp.int32, (count, count), 1
    )
    levels = jnp.sum(jnp.where(diagonal, lev_ref[...], F32(0.0)), axis=1, keepdims=True)
    level = lax.broadcasted_iota(jnp.int32, (count, depth), 0)
    chosen = jnp.where(level == idx_ref[...], levels, F32(0.0))
    values = jnp.sum(chosen, axis=0, keepdims=True)
    live = lax.broadcasted_iota(jnp.int32, (1, depth), 1) < cnt_ref[...]
    weights = jnp.where(live, values, F32(0.0))
    w_own[...] = jnp.broadcast_to(weights, w_own.shape)
    load_picked.wait()
    for h in range(PIECES):
        own_p[h] = e_ref[h * PROWS : (h + 1) * PROWS, :] * weights

    @pl.when(source)
    def _():
        for h in range(PIECES):
            p_buf[own_rel, core, 0, h] = own_p[h]

    load_others.wait()
    for i in range(4):
        span = pl.ds(i * SUB, SUB)
        high, low = split(e_ref[span, :])
        e_hi[span, :depth] = high
        e_lo[span, :depth] = low
    pl.semaphore_wait(barrier, 8)

    def copy(src, dst, send, recv, peer):
        return pltpu.make_async_remote_copy(
            src_ref=src, dst_ref=dst, send_sem=send, recv_sem=recv,
            device_id=peer, device_id_type=MESH,
        )

    def w_copy():
        return copy(w_own, w_in, w_sem.at[0], w_sem.at[1], pair)

    def e_copy(i):
        return copy(e_ref.at[pl.ds(i * PROWS, PROWS)], e_in.at[i], es_sem, er_sem.at[i], pair)

    def slot_of(rel, s, h):
        return p_buf.at[rel, core, s, h], p_sem.at[rel, core, s, h]

    def to_twin(h):
        slot, recv = slot_of(own_rel, 0, h)
        return copy(own_p.at[h], slot, xs_sem, recv, device(dx=2))

    def to_via_x(h):
        peer = pair if h == 2 else other
        return copy(own_p.at[h], via_x.at[h - 1], xs_sem, vx_sem.at[h - 1], peer)

    def from_via_x(h):
        slot, recv = slot_of(own_rel if h == 2 else far_rel, 0, h)
        return copy(via_x.at[h - 1], slot, xs_sem, recv, other if h == 2 else pair)

    def to_source(h):
        slot, recv = slot_of(own_rel, 1, h)
        return copy(own_p.at[h], slot, xs_sem, recv, other)

    def to_via_y(side, h):
        return copy(
            own_p.at[h], via_y.at[side, h], xs_sem, vy_sem.at[side, h],
            device(dy=3 if side == 0 else 1),
        )

    def from_via_y(side, h):
        slot, recv = slot_of(base(1 if side == 0 else 3), 1, h)
        return copy(via_y.at[side, h], slot, xs_sem, recv, other)

    def y_copy(rel, s, h, up):
        slot, recv = slot_of(rel, s, h)
        return copy(slot, slot, ys_sem, recv, device(dy=1 if up else 3))

    def core_copy(rel, s, h):
        slot, recv = slot_of(rel, s, h)
        return copy(slot, slot, cs_sem, recv, device(dcore=1))

    def landed(ref, sem):
        pltpu.make_async_copy(ref, ref, sem).wait()

    def arrive(rel, k, s, h):
        landed(p_buf.at[rel, k, s, h], p_sem.at[rel, k, s, h])

    def spot(rel, k, h):
        odd = lax.rem(rel, 2)
        block = jnp.where(odd == 1, 2 + h, jnp.where(rel == 2, h // 2, 6 + k))
        row = jnp.where(
            odd == 1,
            (rel // 2) * 2 * PROWS + k * PROWS,
            jnp.where(rel == 2, k * 2 * PROWS + lax.rem(h, 2) * PROWS, h * PROWS),
        )
        return block, pl.ds(pl.multiple_of(row, PROWS), PROWS)

    def keep(rel, k, s, h):
        high, low = split(p_buf[rel, k, s, h])
        block, rows_of = spot(rel, k, h)
        p_hi[block, rows_of, s * depth : (s + 1) * depth] = high
        p_lo[block, rows_of, s * depth : (s + 1) * depth] = low

    def sends(rel, s, up):
        gap = row_gap(rel)
        first_hop = gap == 0
        if s == 1:
            first_hop = first_hop & (rel != far_rel)
        if up and s == 0:
            return first_hop | (gap == 3)
        if not up and s == 1:
            return first_hop | (gap == 1)
        return first_hop

    def hand_on(rel, s, h):
        for up in (True, False):
            pl.when(sends(rel, s, up))(lambda up=up: y_copy(rel, s, h, up).start())
        core_copy(rel, s, h).start()
        keep(rel, core, s, h)

    def take(rel, s, h):
        arrive(rel, core, s, h)
        hand_on(rel, s, h)

    def weigh(h, wait=True):
        if wait:
            landed(e_in.at[h], er_sem.at[h])
        p_buf[own_rel, core, 1, h] = e_in[h] * w_in[0:1, :]
        hand_on(own_rel, 1, h)

    def need(rel, h):
        for s in range(2):
            arrive(rel, 1 - core, s, h)
            keep(rel, 1 - core, s, h)

    def need_odd(h):
        need(1, h)
        need(3, h)

    def relay_x(h):
        landed(via_x.at[h - 1], vx_sem.at[h - 1])
        from_via_x(h).start()

    def relay_y(h):
        for side in range(2):
            landed(via_y.at[side, h], vy_sem.at[side, h])
            from_via_y(side, h).start()

    def send_rows(start, stop):
        for i in range(start, stop):
            e_copy(i).start()

    def take_pair(rel, h):
        take(rel, 0, h)
        take(rel, 1, h)

    odd_rel = jnp.where(lax.rem(base(1), 2) == 1, base(1), base(3))
    odd_rel = jnp.where(source, base(2), odd_rel)

    def take_odd(h):
        take_pair(odd_rel, h)
        take_pair(lax.rem(odd_rel + 2, 4), h)

    def begin_source():
        to_twin(0).start()
        to_via_x(1).start()
        to_via_x(3).start()
        w_copy().start()
        send_rows(0, 2)
        to_via_x(2).start()
        send_rows(2, 16)
        hand_on(own_rel, 0, 0)

        @pl.when(source_odd)
        def _():
            hand_on(own_rel, 0, 1)
            landed(w_in, w_sem.at[1])
            weigh(0)
            relay_y(0)
            take(far_rel, 1, 0)
            take(far_rel, 0, 0)
            weigh(1)
            relay_y(1)
            take(far_rel, 1, 1)
            take(far_rel, 0, 1)
            relay_y(2)
            hand_on(own_rel, 0, 2)
            weigh(2)
            relay_y(3)
            landed(e_in.at[3], er_sem.at[3])
            get_rows(0, 4)
            need_odd(0)
            second(0, FIRST)
            need_odd(1)
            second(1, FIRST)
            take(far_rel, 1, 2)
            take(far_rel, 0, 2)
            hand_on(own_rel, 0, 3)
            weigh(3, False)
            need_odd(2)
            second(2, FIRST)
            take(far_rel, 1, 3)
            take(far_rel, 0, 3)
            need_odd(3)
            second(3, FIRST)
            third(0, FIRST)
            third(1, FIRST)
            take_pair(2, 0)
            take_pair(2, 1)
            need(2, 0)
            need(2, 1)
            first(0, FIRST)
            third(2, FIRST)
            third(3, FIRST)
            get_rows(4, 6)
            first(0, SECOND_A)
            second(0, SECOND_A)
            second(1, SECOND_A)
            get_rows(6, 8)
            first(0, SECOND_B)
            second(0, SECOND_B)
            second(1, SECOND_B)
            second(2, SECOND)
            second(3, SECOND)
            for h in (2, 3):
                take_pair(2, h)
                need(2, h)
            first(1, FIRST)
            first(1, SECOND)

        @pl.when(source_even & (own_rel == 2))
        def _():
            hand_on(own_rel, 0, 1)
            landed(w_in, w_sem.at[1])
            weigh(0)
            relay_y(0)
            weigh(1)
            relay_y(1)
            hand_on(own_rel, 0, 2)
            relay_y(2)
            weigh(2)
            relay_y(3)
            hand_on(own_rel, 0, 3)
            weigh(3)
            get_rows(0, 4)
            for two in range(2):
                need(2, 2 * two)
                need(2, 2 * two + 1)
                first(two, FIRST)
            for h in range(PIECES):
                take(far_rel, 1, h)
                take(far_rel, 0, h)

        @pl.when(source_even & (own_rel == 0))
        def _():
            hand_on(own_rel, 0, 1)
            hand_on(own_rel, 0, 2)
            landed(w_in, w_sem.at[1])
            relay_y(0)
            take_pair(far_rel, 0)
            relay_y(1)
            weigh(0)
            take_pair(far_rel, 1)
            relay_y(2)
            relay_y(3)
            for h in range(1, PIECES):
                landed(e_in.at[h], er_sem.at[h])
            get_rows(0, 4)
            need(2, 0)
            need(2, 1)
            first(0, FIRST)
            take_pair(far_rel, 2)
            take_pair(far_rel, 3)
            need(2, 2)
            need(2, 3)
            first(1, FIRST)
            hand_on(own_rel, 0, 3)
            for h in range(1, PIECES):
                weigh(h, False)

        @pl.when(source_even)
        def _():
            get_rows(4, 6)
            first(0, SECOND_A)
            take_odd(0)
            need_odd(0)
            second(0, FIRST)
            second(0, SECOND_A)
            get_rows(6, 8)
            first(0, SECOND_B)
            second(0, SECOND_B)
            first(1, SECOND)
            take_odd(1)
            need_odd(1)
            second(1, FIRST)
            second(1, SECOND_A)
            second(1, SECOND_B)
            third(0, FIRST)
            third(1, FIRST)
            third(0, SECOND_A)
            third(1, SECOND_A)
            get_rows(8, 12)
            first(0, THIRD)
            first(1, THIRD)
            take_odd(2)
            need_odd(2)
            second(2, FIRST)
            second(2, SECOND)

    def begin_bridge():
        for h in range(2):
            to_source(h).start()
        for h in range(PIECES):
            for side in range(2):
                to_via_y(side, h).start()
        w_copy().start()
        send_rows(0, 2)
        relay_x(1)
        send_rows(2, 4)
        relay_x(3)
        send_rows(4, 16)
        for h in range(2, PIECES):
            to_source(h).start()
        odd_next = lax.rem(odd_rel + 2, 4)
        take_pair(odd_rel, 0)
        relay_x(2)
        take_pair(2, 0)
        take_pair(odd_next, 0)
        landed(w_in, w_sem.at[1])
        for i in range(4):
            landed(e_in.at[i], er_sem.at[i])
        get_rows(0, 4)
        need_odd(0)
        second(0, FIRST)
        take_pair(2, 1)
        need(2, 0)
        need(2, 1)
        first(0, FIRST)
        take_pair(odd_rel, 1)
        get_rows(4, 6)
        first(0, SECOND_A)
        second(0, SECOND_A)
        take_pair(odd_next, 1)
        need_odd(1)
        second(1, FIRST)
        second(1, SECOND_A)
        take_pair(2, 2)
        third(0, FIRST)
        third(1, FIRST)
        take_pair(2, 3)
        need(2, 2)
        need(2, 3)
        first(1, FIRST)
    def get_rows(start, stop):
        for i in range(start, stop):
            if start > 0:
                landed(e_in.at[i], er_sem.at[i])
            span = pl.ds(i * PROWS, PROWS)
            high, low = split(e_in[i])
            e_hi[span, depth:] = high
            e_lo[span, depth:] = low

    def dot(a, b):
        return lax.dot_general(a, b, (((1,), (1,)), ((), ())), preferred_element_type=F32)

    def ring(way):
        return (lax.rem(z + 1 + 2 * way, 4) * 2 + xl, r)

    def first_copy(way, two, chunk):
        slots = pl.ds(*chunk)
        return copy(
            part.at[two, slots, pl.ds(2 * way * PROWS, 2 * PROWS)], first_in.at[way, two, slots],
            zs_sem, first_sem.at[way, two, chunk[0]], ring(way),
        )

    def second_copy(way, h, chunk):
        slots = pl.ds(*chunk)
        return copy(
            part.at[2 + h, slots, pl.ds((1 + way) * PROWS, PROWS)], second_in.at[way, h, slots],
            zs_sem, later_sem.at[0, way, h, chunk[0]], ring(way),
        )

    def third_copy(way, h, chunk):
        slots = pl.ds(*chunk)
        return copy(
            part.at[2 + h, slots, pl.ds(3 * way * PROWS, PROWS)], third_in.at[way, h, slots],
            zs_sem, later_sem.at[1, way, h, chunk[0]], ring(way),
        )

    here = z >= 0

    def product(block, chunk):
        span = pl.ds(chunk[0] * WIDE, chunk[1] * WIDE)
        total = dot(p_hi[block], e_hi[span, :])
        total += dot(p_hi[block], e_lo[span, :])
        total += dot(p_lo[block], e_hi[span, :])
        for i in range(chunk[1]):
            part[block, chunk[0] + i] = total[:, i * WIDE : (i + 1) * WIDE]

    def first(two, chunk):
        pl.when(here)(lambda: product(two, chunk))
        for way in range(2):
            first_copy(way, two, chunk).start()

    def second(h, chunk):
        pl.when(here)(lambda: product(2 + h, chunk))
        for way in range(2):
            second_copy(way, h, chunk).start()

    def third(h, chunk):
        slots = pl.ds(*chunk)
        for way in range(2):
            if h % 2 == 0:
                landed(first_in.at[way, h // 2, slots], first_sem.at[way, h // 2, chunk[0]])
            low = (h % 2) * PROWS
            for i in range(chunk[0], chunk[0] + chunk[1]):
                part[2 + h, i, 3 * way * PROWS : (3 * way + 1) * PROWS] += first_in[
                    way, h // 2, i, low : low + PROWS
                ]
            third_copy(way, h, chunk).start()

    def last(chunk):
        pl.when(here)(lambda: product(6, chunk))
        pl.when(here)(lambda: product(7, chunk))

    def finish(h, chunk):
        slots = pl.ds(*chunk)
        for k in range(2):
            landed(second_in.at[1 - k, h, slots], later_sem.at[0, 1 - k, h, chunk[0]])
            landed(third_in.at[k, h, slots], later_sem.at[1, k, h, chunk[0]])
            top = k * SUB + h * PROWS
            for i in range(chunk[0], chunk[0] + chunk[1]):
                total = part[6 + k, i, h * PROWS : (h + 1) * PROWS]
                total += third_in[k, h, i] + second_in[1 - k, h, i]
                out_ref[top : top + PROWS, i * WIDE : (i + 1) * WIDE] = total

    def begin():
        pl.when(source)(begin_source)
        pl.when(bridge)(begin_bridge)

    def more(h):
        @pl.when(bridge if h == 2 else not_odd)
        def _():
            take_odd(h)
            need_odd(h)
            second(h, FIRST)
            second(h, SECOND)

    def pass_own():
        @pl.when(bridge)
        def _():
            for h in range(PIECES):
                take_pair(0, h)

    def own_parts():
        @pl.when(source_odd)
        def _():
            for h in range(PIECES):
                take_pair(0, h)

        for h in range(PIECES):
            need(0, h)

    def middle():
        @pl.when(bridge)
        def _():
            get_rows(6, 8)
            first(0, SECOND_B)
            second(0, SECOND_B)
            first(1, SECOND)
            second(1, SECOND_B)

    def now_third():
        @pl.when(jnp.logical_not(source_even))
        def _():
            third(0, SECOND_A)
            third(1, SECOND_A)

    def now_first():
        @pl.when(jnp.logical_not(source_even))
        def _():
            get_rows(8, 12)
            first(0, THIRD)
            first(1, THIRD)

    def middle_third():
        @pl.when(not_odd)
        def _():
            third(2, FIRST)
            third(3, FIRST)

    begin()
    middle()
    more(2)
    now_third()
    third(0, SECOND_B)
    third(1, SECOND_B)
    now_first()
    more(3)
    pass_own()
    middle_third()
    third(2, SECOND)
    third(3, SECOND)
    for h in range(PIECES):
        second(h, THIRD)
    get_rows(12, 16)
    first(0, FOURTH)
    first(1, FOURTH)
    third(0, THIRD)
    third(1, THIRD)
    second(0, FOURTH)
    third(2, THIRD)
    second(1, FOURTH)
    third(3, THIRD)
    second(2, FOURTH)
    second(3, FOURTH)
    own_parts()
    for chunk in (FIRST, SECOND, THIRD, FOURTH):
        last(chunk)
    for h in range(PIECES):
        third(h, FOURTH)
    for h in range(PIECES):
        for chunk in (FIRST, *((SECOND_A, SECOND_B) if h < 2 else (SECOND,)), THIRD):
            finish(h, chunk)
    for h in range(PIECES):
        finish(h, FOURTH)

    w_copy().wait_send()
    landed(e_ref, es_sem)
    landed(p_buf.at[pl.ds(0, 2)], cs_sem)
    landed(p_buf.at[pl.ds(0, 3)], zs_sem)

    @pl.when(source)
    def _():
        landed(p_buf.at[pl.ds(0, 3), 0, 0], xs_sem)
        landed(p_buf.at[pl.ds(0, 3), 0], ys_sem)

    @pl.when(bridge)
    def _():
        landed(p_buf.at[pl.ds(0, 3), 0, 0], xs_sem)
        landed(via_x, xs_sem)
        landed(p_buf.at[0], ys_sem)


def shards(eigvecs, slice_counts, occ_index, occ_levels):
    rows, depth = eigvecs.shape
    dma = pltpu.SemaphoreType.DMA
    levels = occ_levels.shape[0]
    slots = rows // WIDE
    return pl.pallas_call(
        kernel,
        out_shape=pltpu.VMEM((2 * SUB, rows), F32),
        in_specs=[pl.BlockSpec(memory_space=pl.ANY)] * 4,
        out_specs=pl.BlockSpec(memory_space=pltpu.VMEM),
        scratch_shapes=[
            pltpu.VMEM((rows, depth), F32),
            pltpu.VMEM((1, depth), jnp.int32),
            pltpu.VMEM((1, levels), F32),
            pltpu.VMEM((1, 1), jnp.int32),
            dma((5,)),
            pltpu.VMEM((4, 2, 2, PIECES, PROWS, depth), F32),
            pltpu.VMEM((PIECES, PROWS, depth), F32),
            pltpu.VMEM((PIECES - 1, PROWS, depth), F32),
            pltpu.VMEM((2, PIECES, PROWS, depth), F32),
            pltpu.VMEM((8, depth), F32),
            pltpu.VMEM((8, depth), F32),
            pltpu.VMEM((rows // PROWS, PROWS, depth), F32),
            pltpu.VMEM((8, SUB, 2 * depth), BF16),
            pltpu.VMEM((8, SUB, 2 * depth), BF16),
            pltpu.VMEM((rows, 2 * depth), BF16),
            pltpu.VMEM((rows, 2 * depth), BF16),
            pltpu.VMEM((8, slots, SUB, WIDE), F32),
            pltpu.VMEM((2, 2, slots, 2 * PROWS, WIDE), F32),
            pltpu.VMEM((2, PIECES, slots, PROWS, WIDE), F32),
            pltpu.VMEM((2, PIECES, slots, PROWS, WIDE), F32),
            dma((2,)),
            dma((PIECES - 1,)),
            dma((2, PIECES)),
            dma,
            dma,
            dma,
            dma((4, 2, 2, PIECES)),
            dma,
            dma((rows // PROWS,)),
            dma,
            dma((2, 2, slots)),
            dma((2, 2, PIECES, slots)),
        ],
        compiler_params=pltpu.CompilerParams(
            collective_id=0, has_side_effects=True, vmem_limit_bytes=60 * 1024 * 1024
        ),
    )(
        eigvecs,
        occ_index.reshape(1, depth),
        occ_levels.reshape(1, levels),
        slice_counts.reshape(1, 1),
    )


def solution(mesh):
    return jax.shard_map(
        shards,
        mesh=mesh,
        in_specs=(P("row", "cuts"), P("cuts"), P("cuts"), P()),
        out_specs=P("cuts", "row"),
        check_vma=False,
    )
```

time: 108 us -> 102 us (0.944); the launches traced: 108 us -> 100 us
  Pallas kernels: 106 us -> 98.4 us
    pallas_call x1, Pallas kernels: 106 us -> 98.4 us  [shards(): pl.pallas_call(kernel, out_shape=pltpu.VMEM((2 * SUB, rows), F32), in_spe...]
where the time goes in v4:
time: 102 us; the launch traced here: 100 us
  Pallas kernels  98.4 us (96%)
  local copies, waits for them, and re-layouts  1.32 us (1%)
    pallas_call x1, Pallas kernels, shards(): pl.pallas_call(kernel, out_shape=pltpu.VMEM((2 * SUB, rows), F32), in_spe...  98.4 us

profile of v4, /device:TPU:1, one launch (start us, length us, event | category | flops | bytes accessed | tf_op | source)
XLA Modules:
  0.0 100.4 jit_solution(2589528845813271310)
XLA Ops:
  0.7 98.4 %shard_map.46 = f32[512,1024]{1,0:T(8,128)S(1)} custom-call(f32[1024,512]{1,0:T(8,128)} %e_any.1, s32[1,512]{1,0:T(1,128)} %bitcast.4, f32[1,64]{1,0:T(1,128)} %bitcast.5, s32[1,1]{1,0:T(1,128)} %bitcast.3.cnt_any), custom_call_target="tpu_custom_call" | custom-call | tf_op jit(solution)/shard_map/pallas_call | solution.py:624
  99.0 1.3 %copy.6 = f32[512,1024]{1,0:T(8,128)} copy(f32[512,1024]{1,0:T(8,128)S(1)} %shard_map.46) | data formatting | bytes 4194304

commit v5 on v4

--- a/solution.py
+++ b/solution.py
@@ -12,6 +12,7 @@
 WIDE = 128
 FIRST, SECOND, THIRD, FOURTH = (0, 2), (2, 2), (4, 2), (6, 2)
 SECOND_A, SECOND_B = (2, 1), (3, 1)
+SLOTS = (0, 2, 3, 4, 6)
 F32, BF16 = jnp.float32, jnp.bfloat16
 
 
@@ -96,12 +97,6 @@
         for h in range(PIECES):
             p_buf[own_rel, core, 0, h] = own_p[h]
 
-    load_others.wait()
-    for i in range(4):
-        span = pl.ds(i * SUB, SUB)
-        high, low = split(e_ref[span, :])
-        e_hi[span, :depth] = high
-        e_lo[span, :depth] = low
     pl.semaphore_wait(barrier, 8)
 
     def copy(src, dst, send, recv, peer):
@@ -124,12 +119,11 @@
         return copy(own_p.at[h], slot, xs_sem, recv, device(dx=2))
 
     def to_via_x(h):
-        peer = pair if h == 2 else other
-        return copy(own_p.at[h], via_x.at[h - 1], xs_sem, vx_sem.at[h - 1], peer)
+        return copy(own_p.at[h], via_x.at[h // 2], xs_sem, vx_sem.at[h // 2], other)
 
     def from_via_x(h):
-        slot, recv = slot_of(own_rel if h == 2 else far_rel, 0, h)
-        return copy(via_x.at[h - 1], slot, xs_sem, recv, other if h == 2 else pair)
+        slot, recv = slot_of(far_rel, 0, h)
+        return copy(via_x.at[h // 2], slot, xs_sem, recv, pair)
 
     def to_source(h):
         slot, recv = slot_of(own_rel, 1, h)
@@ -165,7 +159,7 @@
         row = jnp.where(
             odd == 1,
             (rel // 2) * 2 * PROWS + k * PROWS,
-            jnp.where(rel == 2, k * 2 * PROWS + lax.rem(h, 2) * PROWS, h * PROWS),
+            jnp.where(rel == 2, lax.rem(h, 2) * 2 * PROWS + k * PROWS, h * PROWS),
         )
         return block, pl.ds(pl.multiple_of(row, PROWS), PROWS)
 
@@ -212,7 +206,7 @@
         need(3, h)
 
     def relay_x(h):
-        landed(via_x.at[h - 1], vx_sem.at[h - 1])
+        landed(via_x.at[h // 2], vx_sem.at[h // 2])
         from_via_x(h).start()
 
     def relay_y(h):
@@ -234,16 +228,25 @@
     def take_odd(h):
         take_pair(odd_rel, h)
         take_pair(lax.rem(odd_rel + 2, 4), h)
+
+    def send_others():
+        load_others.wait()
+        send_rows(4, 16)
+        for i in range(4):
+            span = pl.ds(i * SUB, SUB)
+            high, low = split(e_ref[span, :])
+            e_hi[span, :depth] = high
+            e_lo[span, :depth] = low
 
     def begin_source():
         to_twin(0).start()
         to_via_x(1).start()
         to_via_x(3).start()
         w_copy().start()
-        send_rows(0, 2)
-        to_via_x(2).start()
-        send_rows(2, 16)
+        send_rows(0, 4)
+        to_twin(2).start()
         hand_on(own_rel, 0, 0)
+        send_others()
 
         @pl.when(source_odd)
         def _():
@@ -273,10 +276,6 @@
             weigh(3, False)
             need_odd(2)
             second(2, FIRST)
-            take(far_rel, 1, 3)
-            take(far_rel, 0, 3)
-            need_odd(3)
-            second(3, FIRST)
             third(0, FIRST)
             third(1, FIRST)
             take_pair(2, 0)
@@ -284,6 +283,10 @@
             need(2, 0)
             need(2, 1)
             first(0, FIRST)
+            take(far_rel, 1, 3)
+            take(far_rel, 0, 3)
+            need_odd(3)
+            second(3, FIRST)
             third(2, FIRST)
             third(3, FIRST)
             get_rows(4, 6)
@@ -321,9 +324,11 @@
                 need(2, 2 * two)
                 need(2, 2 * two + 1)
                 first(two, FIRST)
-            for h in range(PIECES):
-                take(far_rel, 1, h)
-                take(far_rel, 0, h)
+            get_rows(4, 6)
+            first(0, SECOND_A)
+            take_odd(0)
+            for h in range(2):
+                take_pair(far_rel, h)
 
         @pl.when(source_even & (own_rel == 0))
         def _():
@@ -344,22 +349,30 @@
             need(2, 1)
             first(0, FIRST)
             take_pair(far_rel, 2)
-            take_pair(far_rel, 3)
             need(2, 2)
-            need(2, 3)
-            first(1, FIRST)
-            hand_on(own_rel, 0, 3)
-            for h in range(1, PIECES):
-                weigh(h, False)
-
-        @pl.when(source_even)
-        def _():
+            first_one(2, FIRST)
+            weigh(1, False)
             get_rows(4, 6)
             first(0, SECOND_A)
             take_odd(0)
+            take_pair(far_rel, 3)
+            need(2, 3)
+            first_one(3, FIRST)
+            hand_on(own_rel, 0, 3)
+            for h in (2, 3):
+                weigh(h, False)
+
+        @pl.when(source_even)
+        def _():
             need_odd(0)
             second(0, FIRST)
             second(0, SECOND_A)
+
+            @pl.when(own_rel == 2)
+            def _():
+                for h in (2, 3):
+                    take_pair(far_rel, h)
+
             get_rows(6, 8)
             first(0, SECOND_B)
             second(0, SECOND_B)
@@ -389,15 +402,20 @@
                 to_via_y(side, h).start()
         w_copy().start()
         send_rows(0, 2)
-        relay_x(1)
-        send_rows(2, 4)
-        relay_x(3)
-        send_rows(4, 16)
         for h in range(2, PIECES):
             to_source(h).start()
+        load_others.wait()
+        for i in range(4):
+            span = pl.ds(i * SUB, SUB)
+            high, low = split(e_ref[span, :])
+            e_hi[span, :depth] = high
+            e_lo[span, :depth] = low
+        relay_x(1)
+        send_rows(2, 6)
+        relay_x(3)
+        send_rows(6, 16)
         odd_next = lax.rem(odd_rel + 2, 4)
         take_pair(odd_rel, 0)
-        relay_x(2)
         take_pair(2, 0)
         take_pair(odd_next, 0)
         landed(w_in, w_sem.at[1])
@@ -406,25 +424,27 @@
         get_rows(0, 4)
         need_odd(0)
         second(0, FIRST)
+        need(2, 0)
+        first_one(0, FIRST)
         take_pair(2, 1)
-        need(2, 0)
         need(2, 1)
-        first(0, FIRST)
+        first_one(1, FIRST)
         take_pair(odd_rel, 1)
+        take_pair(odd_next, 1)
+        need_odd(1)
+        second(1, FIRST)
         get_rows(4, 6)
         first(0, SECOND_A)
         second(0, SECOND_A)
-        take_pair(odd_next, 1)
-        need_odd(1)
-        second(1, FIRST)
         second(1, SECOND_A)
         take_pair(2, 2)
         third(0, FIRST)
         third(1, FIRST)
+        need(2, 2)
+        first_one(2, FIRST)
         take_pair(2, 3)
-        need(2, 2)
         need(2, 3)
-        first(1, FIRST)
+        first_one(3, FIRST)
     def get_rows(start, stop):
         for i in range(start, stop):
             if start > 0:
@@ -440,73 +460,89 @@
     def ring(way):
         return (lax.rem(z + 1 + 2 * way, 4) * 2 + xl, r)
 
-    def first_copy(way, two, chunk):
+    def first_copy(way, h, chunk):
         slots = pl.ds(*chunk)
         return copy(
-            part.at[two, slots, pl.ds(2 * way * PROWS, 2 * PROWS)], first_in.at[way, two, slots],
-            zs_sem, first_sem.at[way, two, chunk[0]], ring(way),
+            part.at[h // 2, slots, pl.ds((h % 2) * 2 * PROWS + way * PROWS, PROWS)],
+            first_in.at[way, h, slots],
+            zs_sem, first_sem.at[way, h, SLOTS.index(chunk[0])], ring(way),
         )
 
     def second_copy(way, h, chunk):
         slots = pl.ds(*chunk)
         return copy(
             part.at[2 + h, slots, pl.ds((1 + way) * PROWS, PROWS)], second_in.at[way, h, slots],
-            zs_sem, later_sem.at[0, way, h, chunk[0]], ring(way),
+            zs_sem, later_sem.at[0, way, h, SLOTS.index(chunk[0])], ring(way),
         )
 
     def third_copy(way, h, chunk):
         slots = pl.ds(*chunk)
         return copy(
             part.at[2 + h, slots, pl.ds(3 * way * PROWS, PROWS)], third_in.at[way, h, slots],
-            zs_sem, later_sem.at[1, way, h, chunk[0]], ring(way),
+            zs_sem, later_sem.at[1, way, h, SLOTS.index(chunk[0])], ring(way),
         )
 
     here = z >= 0
 
-    def product(block, chunk):
-        span = pl.ds(chunk[0] * WIDE, chunk[1] * WIDE)
-        total = dot(p_hi[block], e_hi[span, :])
-        total += dot(p_hi[block], e_lo[span, :])
-        total += dot(p_lo[block], e_hi[span, :])
+    def product(block, chunk, top=0, count=SUB):
+        span = pl.ds(pl.multiple_of(chunk[0] * WIDE, WIDE), chunk[1] * WIDE)
+        rows_of = pl.ds(top, count)
+        total = dot(p_hi[block, rows_of], e_hi[span, :])
+        total += dot(p_hi[block, rows_of], e_lo[span, :])
+        total += dot(p_lo[block, rows_of], e_hi[span, :])
         for i in range(chunk[1]):
-            part[block, chunk[0] + i] = total[:, i * WIDE : (i + 1) * WIDE]
+            part[block, chunk[0] + i, rows_of] = total[:, i * WIDE : (i + 1) * WIDE]
 
     def first(two, chunk):
         pl.when(here)(lambda: product(two, chunk))
+        for h in (2 * two, 2 * two + 1):
+            for way in range(2):
+                first_copy(way, h, chunk).start()
+
+    def first_one(h, chunk):
+        pl.when(here)(lambda: product(h // 2, chunk, (h % 2) * 2 * PROWS, 2 * PROWS))
         for way in range(2):
-            first_copy(way, two, chunk).start()
+            first_copy(way, h, chunk).start()
 
     def second(h, chunk):
         pl.when(here)(lambda: product(2 + h, chunk))
         for way in range(2):
             second_copy(way, h, chunk).start()
 
+    def second_all(chunk):
+        def step(h, carry):
+            product(2 + h, chunk)
+            for way in range(2):
+                second_copy(way, h, chunk).start()
+            return carry
+
+        lax.fori_loop(0, PIECES, step, 0)
+
     def third(h, chunk):
         slots = pl.ds(*chunk)
         for way in range(2):
-            if h % 2 == 0:
-                landed(first_in.at[way, h // 2, slots], first_sem.at[way, h // 2, chunk[0]])
-            low = (h % 2) * PROWS
+            landed(first_in.at[way, h, slots], first_sem.at[way, h, SLOTS.index(chunk[0])])
             for i in range(chunk[0], chunk[0] + chunk[1]):
-                part[2 + h, i, 3 * way * PROWS : (3 * way + 1) * PROWS] += first_in[
-                    way, h // 2, i, low : low + PROWS
-                ]
+                part[2 + h, i, 3 * way * PROWS : (3 * way + 1) * PROWS] += first_in[way, h, i]
             third_copy(way, h, chunk).start()
 
-    def last(chunk):
-        pl.when(here)(lambda: product(6, chunk))
-        pl.when(here)(lambda: product(7, chunk))
+    def last_parts():
+        def step(n, carry):
+            product(6 + n // 4, (lax.rem(n, 4) * 2, 2))
+            return carry
+
+        lax.fori_loop(0, 8, step, 0)
 
     def finish(h, chunk):
         slots = pl.ds(*chunk)
         for k in range(2):
-            landed(second_in.at[1 - k, h, slots], later_sem.at[0, 1 - k, h, chunk[0]])
-            landed(third_in.at[k, h, slots], later_sem.at[1, k, h, chunk[0]])
-            top = k * SUB + h * PROWS
+            landed(second_in.at[1 - k, h, slots], later_sem.at[0, 1 - k, h, SLOTS.index(chunk[0])])
+            landed(third_in.at[k, h, slots], later_sem.at[1, k, h, SLOTS.index(chunk[0])])
+            piece = pl.ds(pl.multiple_of(h * PROWS, PROWS), PROWS)
+            rows_of = pl.ds(pl.multiple_of(k * SUB + h * PROWS, PROWS), PROWS)
             for i in range(chunk[0], chunk[0] + chunk[1]):
-                total = part[6 + k, i, h * PROWS : (h + 1) * PROWS]
-                total += third_in[k, h, i] + second_in[1 - k, h, i]
-                out_ref[top : top + PROWS, i * WIDE : (i + 1) * WIDE] = total
+                total = part[6 + k, i, piece] + (third_in[k, h, i] + second_in[1 - k, h, i])
+                out_ref[rows_of, i * WIDE : (i + 1) * WIDE] = total
 
     def begin():
         pl.when(source)(begin_source)
@@ -575,8 +611,7 @@
     middle_third()
     third(2, SECOND)
     third(3, SECOND)
-    for h in range(PIECES):
-        second(h, THIRD)
+    second_all(THIRD)
     get_rows(12, 16)
     first(0, FOURTH)
     first(1, FOURTH)
@@ -589,15 +624,21 @@
     second(2, FOURTH)
     second(3, FOURTH)
     own_parts()
-    for chunk in (FIRST, SECOND, THIRD, FOURTH):
-        last(chunk)
+    last_parts()
     for h in range(PIECES):
         third(h, FOURTH)
-    for h in range(PIECES):
-        for chunk in (FIRST, *((SECOND_A, SECOND_B) if h < 2 else (SECOND,)), THIRD):
-            finish(h, chunk)
-    for h in range(PIECES):
-        finish(h, FOURTH)
+    def finish_all(start, stop, chunks):
+        def step(h, carry):
+            for chunk in chunks:
+                finish(h, chunk)
+            return carry
+
+        lax.fori_loop(start, stop, step, 0)
+
+    finish_all(0, 2, (FIRST, SECOND_A, SECOND_B))
+    finish_all(2, 4, (FIRST, SECOND))
+    finish_all(0, 4, (THIRD,))
+    finish_all(0, 4, (FOURTH,))
 
     w_copy().wait_send()
     landed(e_ref, es_sem)
@@ -634,7 +675,7 @@
             dma((5,)),
             pltpu.VMEM((4, 2, 2, PIECES, PROWS, depth), F32),
             pltpu.VMEM((PIECES, PROWS, depth), F32),
-            pltpu.VMEM((PIECES - 1, PROWS, depth), F32),
+            pltpu.VMEM((2, PROWS, depth), F32),
             pltpu.VMEM((2, PIECES, PROWS, depth), F32),
             pltpu.VMEM((8, depth), F32),
             pltpu.VMEM((8, depth), F32),
@@ -644,11 +685,11 @@
             pltpu.VMEM((rows, 2 * depth), BF16),
             pltpu.VMEM((rows, 2 * depth), BF16),
             pltpu.VMEM((8, slots, SUB, WIDE), F32),
-            pltpu.VMEM((2, 2, slots, 2 * PROWS, WIDE), F32),
+            pltpu.VMEM((2, PIECES, slots, PROWS, WIDE), F32),
             pltpu.VMEM((2, PIECES, slots, PROWS, WIDE), F32),
             pltpu.VMEM((2, PIECES, slots, PROWS, WIDE), F32),
             dma((2,)),
-            dma((PIECES - 1,)),
+            dma((2,)),
             dma((2, PIECES)),
             dma,
             dma,
@@ -657,8 +698,8 @@
             dma,
             dma((rows // PROWS,)),
             dma,
-            dma((2, 2, slots)),
-            dma((2, 2, PIECES, slots)),
+            dma((2, PIECES, len(SLOTS))),
+            dma((2, 2, PIECES, len(SLOTS))),
         ],
         compiler_params=pltpu.CompilerParams(
             collective_id=0, has_side_effects=True, vmem_limit_bytes=60 * 1024 * 1024

time: 102 us -> 101 us (level); the launches traced: 100 us -> 101 us
  no operation moved by 1% of the time
where the time goes in v5:
time: 101 us
  Pallas kernels  98.8 us (98%)
  local copies, waits for them, and re-layouts  1.32 us (1%)
    pallas_call x1, Pallas kernels, shards(): pl.pallas_call(kernel, out_shape=pltpu.VMEM((2 * SUB, rows), F32), in_spe...  98.8 us

profile of v5, /device:TPU:1, one launch (start us, length us, event | category | flops | bytes accessed | tf_op | source)
XLA Modules:
  0.0 100.8 jit_solution(16319978965931803496)
XLA Ops:
  0.7 98.8 %shard_map.46 = f32[512,1024]{1,0:T(8,128)S(1)} custom-call(f32[1024,512]{1,0:T(8,128)} %e_any.1, s32[1,512]{1,0:T(1,128)} %bitcast.4, f32[1,64]{1,0:T(1,128)} %bitcast.5, s32[1,1]{1,0:T(1,128)} %bitcast.3.cnt_any), custom_call_target="tpu_custom_call" | custom-call | tf_op jit(solution)/shard_map/pallas_call | solution.py:665
  99.4 1.3 %copy.6 = f32[512,1024]{1,0:T(8,128)} copy(f32[512,1024]{1,0:T(8,128)S(1)} %shard_map.46) | data formatting | bytes 4194304

commit v6 on v5

--- a/solution.py
+++ b/solution.py
@@ -22,8 +22,8 @@
 
 
 def kernel(
-    e_any, idx_any, lev_any, cnt_any, out_ref,
-    e_ref, idx_ref, lev_ref, cnt_ref, in_sem, p_buf, own_p, via_x, via_y, w_own, w_in, e_in, p_hi, p_lo, e_hi, e_lo, part, first_in, second_in, third_in,
+    e_any, idx_any, lev_any, cnt_any, out_any,
+    out_ref, out_sem, e_ref, idx_ref, lev_ref, cnt_ref, in_sem, p_buf, own_p, via_x, via_y, w_own, w_in, e_in, p_hi, p_lo, e_hi, e_lo, part, first_in, second_in, third_in,
     w_sem, vx_sem, vy_sem, xs_sem, ys_sem, cs_sem, p_sem, es_sem, er_sem, zs_sem, first_sem, later_sem,
 ):
     rows, depth = e_ref.shape
@@ -465,21 +465,21 @@
         return copy(
             part.at[h // 2, slots, pl.ds((h % 2) * 2 * PROWS + way * PROWS, PROWS)],
             first_in.at[way, h, slots],
-            zs_sem, first_sem.at[way, h, SLOTS.index(chunk[0])], ring(way),
+            zs_sem, first_sem.at[h, SLOTS.index(chunk[0])], ring(way),
         )
 
     def second_copy(way, h, chunk):
         slots = pl.ds(*chunk)
         return copy(
             part.at[2 + h, slots, pl.ds((1 + way) * PROWS, PROWS)], second_in.at[way, h, slots],
-            zs_sem, later_sem.at[0, way, h, SLOTS.index(chunk[0])], ring(way),
+            zs_sem, later_sem.at[0, h, SLOTS.index(chunk[0])], ring(way),
         )
 
     def third_copy(way, h, chunk):
         slots = pl.ds(*chunk)
         return copy(
             part.at[2 + h, slots, pl.ds(3 * way * PROWS, PROWS)], third_in.at[way, h, slots],
-            zs_sem, later_sem.at[1, way, h, SLOTS.index(chunk[0])], ring(way),
+            zs_sem, later_sem.at[1, h, SLOTS.index(chunk[0])], ring(way),
         )
 
     here = z >= 0
@@ -520,8 +520,8 @@
 
     def third(h, chunk):
         slots = pl.ds(*chunk)
+        landed(first_in.at[:, h, slots], first_sem.at[h, SLOTS.index(chunk[0])])
         for way in range(2):
-            landed(first_in.at[way, h, slots], first_sem.at[way, h, SLOTS.index(chunk[0])])
             for i in range(chunk[0], chunk[0] + chunk[1]):
                 part[2 + h, i, 3 * way * PROWS : (3 * way + 1) * PROWS] += first_in[way, h, i]
             third_copy(way, h, chunk).start()
@@ -535,9 +535,9 @@
 
     def finish(h, chunk):
         slots = pl.ds(*chunk)
+        landed(second_in.at[:, h, slots], later_sem.at[0, h, SLOTS.index(chunk[0])])
+        landed(third_in.at[:, h, slots], later_sem.at[1, h, SLOTS.index(chunk[0])])
         for k in range(2):
-            landed(second_in.at[1 - k, h, slots], later_sem.at[0, 1 - k, h, SLOTS.index(chunk[0])])
-            landed(third_in.at[k, h, slots], later_sem.at[1, k, h, SLOTS.index(chunk[0])])
             piece = pl.ds(pl.multiple_of(h * PROWS, PROWS), PROWS)
             rows_of = pl.ds(pl.multiple_of(k * SUB + h * PROWS, PROWS), PROWS)
             for i in range(chunk[0], chunk[0] + chunk[1]):
@@ -635,11 +635,22 @@
 
         lax.fori_loop(start, stop, step, 0)
 
+    def put(rows_of, columns):
+        pltpu.make_async_copy(
+            out_ref.at[rows_of, columns], out_any.at[rows_of, columns], out_sem
+        ).start()
+
     finish_all(0, 2, (FIRST, SECOND_A, SECOND_B))
     finish_all(2, 4, (FIRST, SECOND))
+    put(pl.ds(0, 2 * SUB), pl.ds(0, 4 * WIDE))
     finish_all(0, 4, (THIRD,))
-    finish_all(0, 4, (FOURTH,))
-
+    put(pl.ds(0, 2 * SUB), pl.ds(4 * WIDE, 2 * WIDE))
+    for h in range(PIECES):
+        finish(h, FOURTH)
+        for k in range(2):
+            put(pl.ds(k * SUB + h * PROWS, PROWS), pl.ds(6 * WIDE, 2 * WIDE))
+
+    pltpu.make_async_copy(out_ref, out_any, out_sem).wait()
     w_copy().wait_send()
     landed(e_ref, es_sem)
     landed(p_buf.at[pl.ds(0, 2)], cs_sem)
@@ -666,8 +677,10 @@
         kernel,
         out_shape=pltpu.VMEM((2 * SUB, rows), F32),
         in_specs=[pl.BlockSpec(memory_space=pl.ANY)] * 4,
-        out_specs=pl.BlockSpec(memory_space=pltpu.VMEM),
+        out_specs=pl.BlockSpec(memory_space=pl.ANY),
         scratch_shapes=[
+            pltpu.VMEM((2 * SUB, rows), F32),
+            dma,
             pltpu.VMEM((rows, depth), F32),
             pltpu.VMEM((1, depth), jnp.int32),
             pltpu.VMEM((1, levels), F32),
@@ -698,8 +711,8 @@
             dma,
             dma((rows // PROWS,)),
             dma,
+            dma((PIECES, len(SLOTS))),
             dma((2, PIECES, len(SLOTS))),
-            dma((2, 2, PIECES, len(SLOTS))),
         ],
         compiler_params=pltpu.CompilerParams(
             collective_id=0, has_side_effects=True, vmem_limit_bytes=60 * 1024 * 1024

time: 101 us -> 100 us (0.990)
  no operation moved by 1% of the time
where the time goes in v6:
time: 100 us
  Pallas kernels  98.3 us (98%)
  local copies, waits for them, and re-layouts  1.32 us (1%)
    pallas_call x1, Pallas kernels, shards(): pl.pallas_call(kernel, out_shape=pltpu.VMEM((2 * SUB, rows), F32), in_spe...  98.3 us

profile of v6, /device:TPU:1, one launch (start us, length us, event | category | flops | bytes accessed | tf_op | source)
XLA Modules:
  0.0 100.3 jit_solution(6078383472894096572)
XLA Ops:
  0.7 98.3 %shard_map.46 = f32[512,1024]{1,0:T(8,128)S(1)} custom-call(f32[1024,512]{1,0:T(8,128)} %e_any.1, s32[1,512]{1,0:T(1,128)} %bitcast.4, f32[1,64]{1,0:T(1,128)} %bitcast.5, s32[1,1]{1,0:T(1,128)} %bitcast.3.cnt_any), custom_call_target="tpu_custom_call" | custom-call | tf_op jit(solution)/shard_map/pallas_call | solution.py:676
  98.9 1.3 %copy.6 = f32[512,1024]{1,0:T(8,128)} copy(f32[512,1024]{1,0:T(8,128)S(1)} %shard_map.46) | data formatting | bytes 4194304

commit v7 on v6

--- a/solution.py
+++ b/solution.py
@@ -254,12 +254,12 @@
             landed(w_in, w_sem.at[1])
             weigh(0)
             relay_y(0)
+            take(far_rel, 0, 0)
             take(far_rel, 1, 0)
-            take(far_rel, 0, 0)
             weigh(1)
             relay_y(1)
+            take(far_rel, 0, 1)
             take(far_rel, 1, 1)
-            take(far_rel, 0, 1)
             relay_y(2)
             hand_on(own_rel, 0, 2)
             weigh(2)
@@ -270,8 +270,8 @@
             second(0, FIRST)
             need_odd(1)
             second(1, FIRST)
+            take(far_rel, 0, 2)
             take(far_rel, 1, 2)
-            take(far_rel, 0, 2)
             hand_on(own_rel, 0, 3)
             weigh(3, False)
             need_odd(2)
@@ -283,8 +283,8 @@
             need(2, 0)
             need(2, 1)
             first(0, FIRST)
+            take(far_rel, 0, 3)
             take(far_rel, 1, 3)
-            take(far_rel, 0, 3)
             need_odd(3)
             second(3, FIRST)
             third(2, FIRST)

time: 100 us -> 100 us (level)
  no operation moved by 1% of the time
where the time goes in v7:
time: 100 us
  Pallas kernels  98.3 us (98%)
  local copies, waits for them, and re-layouts  1.32 us (1%)
    pallas_call x1, Pallas kernels, shards(): pl.pallas_call(kernel, out_shape=pltpu.VMEM((2 * SUB, rows), F32), in_spe...  98.3 us

profile of v7, /device:TPU:1, one launch (start us, length us, event | category | flops | bytes accessed | tf_op | source)
XLA Modules:
  0.0 100.3 jit_solution(4090541015100553992)
XLA Ops:
  0.7 98.3 %shard_map.46 = f32[512,1024]{1,0:T(8,128)S(1)} custom-call(f32[1024,512]{1,0:T(8,128)} %e_any.1, s32[1,512]{1,0:T(1,128)} %bitcast.4, f32[1,64]{1,0:T(1,128)} %bitcast.5, s32[1,1]{1,0:T(1,128)} %bitcast.3.cnt_any), custom_call_target="tpu_custom_call" | custom-call | tf_op jit(solution)/shard_map/pallas_call | solution.py:676
  99.0 1.3 %copy.6 = f32[512,1024]{1,0:T(8,128)} copy(f32[512,1024]{1,0:T(8,128)S(1)} %shard_map.46) | data formatting | bytes 4194304
